TPU v7x, 32 devices: a whole 2x2x4 slice. The times are simulated.
32 devices in a mesh: first: 8 (over z, core), second: 4 (over y, x).
Axes of the slice: x: 2, y: 2, z: 4, core: 2. Of those that a mesh axis runs over, the one named last changes fastest.
Arguments:
- pair_rows: bfloat16 [96, 96, 128], P('first', 'second'), may hold values from -6 to 6
- in_gain: float32 [128], replicated, may hold values from 0.25 to 1.75
- left_weight: bfloat16 [128, 128], replicated, may hold values from -0.5 to 0.5
- right_weight: bfloat16 [128, 128], replicated, may hold values from -0.5 to 0.5
- mid_gain: float32 [128], replicated, may hold values from 0.25 to 1.75
- out_weight: bfloat16 [128, 128], replicated, may hold values from -0.5 to 0.5
- out_gate: bfloat16 [128, 128], replicated, may hold values from -0.5 to 0.5
Outputs:
- triangle_out: bfloat16 [96, 96, 128], P('first', 'second')
All inputs are finite; a program needn't handle non-finite values.
Results may differ from a plain program's by a relative error of at most 0.012.
Values may be sent and summed in bfloat16 or wider, within the bound.
No kernel may reach another device: no remote copies, remote signals or barrier semaphores. Data moves between devices by JAX's collectives and lax.ppermute only.
A program may use at most 64 MiB of HBM per device.

v0:
```python
import functools
import math

import jax
import jax.numpy as jnp
from jax import lax
from jax.experimental import pallas as pl
from jax.experimental.pallas import tpu as pltpu
from jax.sharding import PartitionSpec as P


EARLY, LATE, ORDER = 1, [2, 3], [3, 1, 2]
VMEM = pl.BlockSpec(memory_space=pltpu.VMEM)


def norm_channels(values, channel_gain):
    centred = values - jnp.mean(values, axis=-1, keepdims=True)
    variance = jnp.mean(centred * centred, axis=-1, keepdims=True)
    return centred * lax.rsqrt(variance + 1e-05) * channel_gain


def dot(rows, weight):
    return jnp.dot(rows, weight, preferred_element_type=jnp.float32)


def project(rows, gain, weight):
    ready = norm_channels(rows.astype(jnp.float32), gain).astype(jnp.bfloat16)
    return dot(ready, weight).astype(jnp.bfloat16).astype(jnp.float32)


def core_of():
    return lax.rem(lax.axis_index("first"), 2)


def cut(block, upper, flat, at):
    half = block.shape[1] // 2
    for k in range(block.shape[0]):
        row = block[k].astype(jnp.float32)
        flat[pl.ds(at + k * half, half)] = jnp.where(upper, row[half:], row[:half])


def pack_kernel(mine, other, out, flat):
    upper = core_of() == 1
    cut(mine, upper, flat, 0)
    cut(other, upper, flat, flat.shape[0] // 2)
    out[...] = flat[...].astype(out.dtype)


def split_kernel(block, kept, passed, flat):
    cut(block, core_of() == 1, flat, 0)
    kept[...] = flat[...].astype(kept.dtype)
    cut(block, core_of() == 0, flat, 0)
    passed[...] = flat[...].astype(passed.dtype)


def load_kernel(*refs):
    count = len(refs) // 2
    copies = [
        pltpu.make_async_copy(source, target, refs[-1].at[i])
        for i, (source, target) in enumerate(zip(refs[:count], refs[count:-1]))
    ]
    for copy in copies:
        copy.start()
    for copy in copies:
        copy.wait()


def gate_kernel(mine, gain, weight, out):
    rows, columns, width = mine.shape
    flat = mine[...].reshape(rows * columns, width).astype(jnp.float32)
    ready = norm_channels(flat, gain[...]).astype(jnp.bfloat16)
    out[...] = jax.nn.sigmoid(dot(ready, weight[...])).reshape(rows, columns, -1)


def add_block(left, right, sums, place):
    depth, columns, width = right.shape
    half = left.shape[0] // depth
    group = max(g for g in range(1, half + 1) if half % g == 0 and g * columns <= 288)
    for base in range(0, half, group):

        def step(k, totals):
            line = right[k]
            return tuple(
                total + left[pl.ds(k * half + base + i, 1)] * line
                for i, total in enumerate(totals)
            )

        totals = (jnp.zeros((columns, width), jnp.float32),) * group
        totals = lax.fori_loop(0, depth, step, totals, unroll=6)
        for i, total in enumerate(totals):
            sums[place, base + i] = total


def first_kernel(kept, mine, other, gain, left_weight, right_weight, right, sums, left):
    rows, columns, width = mine.shape
    for part, block in enumerate((mine, other)):
        flat = project(block[...].reshape(rows * columns, width), gain[...], right_weight[...])
        right[pl.ds(part * rows, rows)] = flat.reshape(rows, columns, -1)
    left[...] = project(kept[...], gain[...], left_weight[...])
    add_block(left, right, sums, lax.axis_index("second"))


def middle_kernel(steps, *refs):
    (right, gain, weight, _, sums, left) = refs[len(steps) :]
    for step, block in zip(steps, refs):
        left[...] = project(block[...], gain[...], weight[...])
        add_block(left, right, sums, lax.axis_index("second") ^ step)


def joined_kernel(step, kept, passed, right, gain, weight, _, sums, left):
    rows = kept.shape[0]
    for part, block in enumerate((kept, passed)):
        left[pl.ds(part * rows, rows)] = project(block[...], gain[...], weight[...])
    add_block(left, right, sums, lax.axis_index("second") ^ step)


def last_kernel(step, messages, merge, block, right, gain, weight, before, *refs):
    *outs, sums, left = refs
    first, second = lax.axis_index("first"), lax.axis_index("second")
    chip, core = first // 2, lax.rem(first, 2)
    left[...] = project(block[...], gain[...], weight[...])
    add_block(left, right, sums, second ^ step)
    for out, (chips, cores) in zip(outs, messages):
        place = (chip ^ chips) if merge == 1 else 2 * (chip ^ chips) + (core ^ cores)
        out[...] = sums[place].astype(out.dtype)


def final_kernel(merge, per, scale, *refs):
    parts, (gate, gain, weight, out) = refs[:-4], refs[-4:]
    core = core_of()
    half, columns, width = parts[0].shape
    for slot in range(merge):
        mine = parts[slot * per : (slot + 1) * per]
        total = sum(part[...].astype(jnp.float32) for part in mine)
        flat = total.reshape(half * columns, width) * scale
        scaled = norm_channels(flat, gain[...]).astype(jnp.bfloat16)
        result = dot(scaled, weight[...]).reshape(half, columns, -1)
        rows = pl.ds(0, half) if merge == 1 else pl.ds((core ^ slot) * half, half)
        out[rows] = (result * gate[rows]).astype(out.dtype)


def call(kernel, out_shapes, *operands, scratch=(), waits=(), aliases={}, space=pltpu.VMEM):
    many = isinstance(out_shapes, list)
    held = jax.tree.leaves(out_shapes) + list(operands) + list(scratch)
    held = sum(math.prod(ref.shape) * jnp.dtype(ref.dtype).itemsize for ref in held)
    return pl.pallas_call(
        kernel,
        out_shape=out_shapes,
        in_specs=[pl.BlockSpec(memory_space=space)] * len(operands),
        out_specs=[VMEM] * len(out_shapes) if many else VMEM,
        scratch_shapes=[*scratch, *waits],
        input_output_aliases=aliases,
        compiler_params=pltpu.CompilerParams(vmem_limit_bytes=held + (2 << 20)),
        cost_estimate=pl.CostEstimate(
            flops=1 << 24, bytes_accessed=100000, transcendentals=0
        ),
    )(*operands)


def shards(pair_rows, in_gain, left_weight, right_weight, mid_gain, out_weight, out_gate):
    firsts, seconds = lax.axis_size("first"), lax.axis_size("second")
    rows, columns, width = pair_rows.shape
    mix, wide = left_weight.shape[1], out_weight.shape[1]
    chips, half, depth = firsts // 2, columns // 2, 2 * rows
    merge = rows // half
    in_gain, mid_gain = in_gain.reshape(1, -1), mid_gain.reshape(1, -1)
    axes = ("first", "second")
    shape, f32 = jax.ShapeDtypeStruct, jnp.float32

    def swap(values, chip=0, core=0, block=0):
        pairs = [
            (a * seconds + b, (a ^ (2 * chip + core)) * seconds + (b ^ block))
            for a in range(firsts)
            for b in range(seconds)
        ]
        return lax.ppermute(values, axes, pairs)

    lefts = [pltpu.VMEM((depth * half, mix), f32)]
    held = shape((seconds, half, columns, mix), f32)
    flat = shape((depth * half, width), pair_rows.dtype)
    part = shape((rows * half, width), pair_rows.dtype)
    other = swap(pair_rows, core=1)
    early = swap(pair_rows, block=EARLY)
    arguments = (
        pair_rows,
        in_gain,
        right_weight,
        out_gate,
        left_weight,
        mid_gain,
        out_weight,
    )
    mine, in_gain, right_weight, out_gate, left_weight, mid_gain, out_weight = call(
        load_kernel,
        [shape(x.shape, x.dtype) for x in arguments],
        *[pltpu.with_memory_space_constraint(x, pltpu.HBM) for x in arguments],
        waits=[pltpu.SemaphoreType.DMA((len(arguments),))],
        space=pltpu.HBM,
    )
    kept = call(pack_kernel, flat, mine, other, scratch=[pltpu.VMEM(flat.shape, f32)])
    late = [s for s in range(1, seconds) if s != EARLY]
    if seconds == 4:
        late = LATE
    blocks = [swap(kept, block=s) for s in late[:-1]]
    last = swap(kept, block=late[-1])
    right, sums = call(
        first_kernel,
        [shape((depth, columns, mix), f32), held],
        kept,
        mine,
        other,
        in_gain,
        left_weight,
        right_weight,
        scratch=lefts,
    )
    factors = (right, in_gain, left_weight)
    near, passed = call(split_kernel, [part, part], early, scratch=[pltpu.VMEM(part.shape, f32)])
    passed = swap(passed, core=1)
    sums = call(
        functools.partial(middle_kernel, late[:-1]),
        held,
        *blocks,
        *factors,
        sums,
        scratch=lefts,
        aliases={len(blocks) + 3: 0},
    )
    sums = call(
        functools.partial(joined_kernel, EARLY),
        held,
        near,
        passed,
        *factors,
        sums,
        scratch=lefts,
        aliases={5: 0},
    )
    cores = range(merge)
    order = ORDER if chips == 4 else list(range(1, chips))
    messages = [(t, c) for t in order + [0] for c in reversed(cores)]
    *outgoing, _ = call(
        functools.partial(last_kernel, late[-1], messages, merge),
        [shape((half, columns, mix), f32 if m == (0, 0) else jnp.bfloat16) for m in messages]
        + [held],
        last,
        *factors,
        sums,
        scratch=lefts,
        aliases={4: len(messages)},
    )
    gate = call(gate_kernel, shape((rows, columns, wide), f32), mine, in_gain, out_gate)
    arrived = {
        (t, c): sent if (t, c) == (0, 0) else swap(sent, chip=t, core=c)
        for (t, c), sent in zip(messages, outgoing)
    }
    parts = [arrived[t, c] for c in cores for t in [0] + order]
    return call(
        functools.partial(final_kernel, merge, chips, (rows * firsts) ** -0.5),
        shape((rows, columns, wide), jnp.bfloat16),
        *parts,
        gate,
        mid_gain,
        out_weight,
    )


def solution(mesh):
    in_specs = (P("first", "second", None), P(), P(), P(), P(), P(), P())
    out_specs = P("first", "second", None)
    return jax.shard_map(shards, mesh=mesh, in_specs=in_specs, out_specs=out_specs, check_vma=False)
```

profile of v0, /device:TPU:0, one launch (start us, length us, event | category | flops | bytes accessed | tf_op | source)
XLA Modules:
  0.0 21.4 jit_solution(627707749017193679)
XLA Ops:
  0.0 0.5 %collective-permute-start = (bf16[12,24,128]{2,1,0:T(8,128)(2,1)}, bf16[12,24,128]{2,1,0:T(8,128)(2,1)S(1)}, u32[]{:S(2)}, u32[]{:S(2)}) collective-permute-start(bf16[12,24,128]{2,1,0:T(8,128)(2,1)} %refs_0_.1), channel_id=1, source_target_pairs={{0,4},{1,5},{2,6},{3,7},{4,0},{5,1},{6,2},{7,3},{8,12},{9,13},{10,... | collective-permute-start | bytes 221192 | tf_op jit(solution)/shard_map/ppermute | solution.py:176
  0.5 2.5 %collective-permute-start.2 = (bf16[12,24,128]{2,1,0:T(8,128)(2,1)}, bf16[12,24,128]{2,1,0:T(8,128)(2,1)S(1)}, u32[]{:S(2)}, u32[]{:S(2)}) collective-permute-start(bf16[12,24,128]{2,1,0:T(8,128)(2,1)} %refs_0_.1), channel_id=1, source_target_pairs={{0,1},{1,0},{2,3},{3,2},{4,5},{5,4},{6,7},{7,6},{8,9},{9,8},{10,11... | collective-permute-start | bytes 221192 | tf_op jit(solution)/shard_map/ppermute | solution.py:176
  3.0 1.0 %shard_map.73 = (bf16[12,24,128]{2,1,0:T(8,128)(2,1)S(1)}, f32[1,128]{1,0:T(1,128)S(1)}, bf16[128,128]{1,0:T(8,128)(2,1)S(1)}, bf16[128,128]{1,0:T(8,128)(2,1)S(...) custom-call(bf16[12,24,128]{2,1,0:T(8,128)(2,1)} %refs_0_.1, ...), custom_call_target="tpu_custom_call" | custom-call | flops 16777216 | bytes 100000 | tf_op jit(solution)/shard_map/pallas_call | solution.py:146
  4.0 0.0 collective-permute-done.other
  4.0 1.6 %collective-permute-start.4 = (bf16[288,128]{1,0:T(8,128)(2,1)S(1)}, bf16[288,128]{1,0:T(8,128)(2,1)S(1)}, u32[]{:S(2)}, u32[]{:S(2)}) collective-permute-start(bf16[288,128]{1,0:T(8,128)(2,1)S(1)} %shard_map.74.kept), channel_id=1, source_target_pairs={{0,2},{1,3},{2,0},{3,1},{4,6},{5,7},{6,4},{7,5},{8,10},{9,11},{10,... | collective-permute-start | bytes 221192 | tf_op jit(solution)/shard_map/ppermute | solution.py:176
  5.6 0.4 %collective-permute-start.1 = (bf16[288,128]{1,0:T(8,128)(2,1)S(1)}, bf16[288,128]{1,0:T(8,128)(2,1)S(1)}, u32[]{:S(2)}, u32[]{:S(2)}) collective-permute-start(bf16[288,128]{1,0:T(8,128)(2,1)S(1)} %shard_map.74.kept), channel_id=1, source_target_pairs={{0,3},{1,2},{2,1},{3,0},{4,7},{5,6},{6,5},{7,4},{8,11},{9,10},{10,... | collective-permute-start | bytes 221192 | tf_op jit(solution)/shard_map/ppermute | solution.py:176
  6.0 0.1 collective-permute-done.2.block
  6.2 0.1 collective-permute-start.3
  6.2 0.7 %shard_map.75 = (f32[24,24,128]{2,1,0:T(8,128)S(1)}, f32[4,12,24,128]{3,2,1,0:T(8,128)S(1)}) custom-call(bf16[288,128]{1,0:T(8,128)(2,1)S(1)} %shard_map.74.kept, bf16[12,24,128]{2,1,0:T(8,128)(2,1)S(1)} %get-tuple-element.20.mine, bf16[12,24,128]{2,1,0:T(8,128)(2,1)S(1)} %collective-permute-done.other, f32[1,128]{1,0:T(1,128)S(1)} %get-tuple-element.21.gain.refs_2_, ...), custom_call_target="tpu_custom_call" | custom-call | flops 16777216 | bytes 100000 | tf_op jit(solution)/shard_map/pallas_call | solution.py:146
  6.9 2.2 %collective-permute-done.4.refs_0_ = bf16[288,128]{1,0:T(8,128)(2,1)S(1)} collective-permute-done((bf16[288,128]{1,0:T(8,128)(2,1)S(1)}, bf16[288,128]{1,0:T(8,128)(2,1)S(1)}, u32[]{:S(2)}, u32[]{:S(2)}) %collective-permute-start.4) | collective-permute-done | bytes 73760 | tf_op jit(solution)/shard_map/ppermute | solution.py:176
  9.1 0.6 %shard_map.77._ = f32[4,12,24,128]{3,2,1,0:T(8,128)S(1)} custom-call(bf16[288,128]{1,0:T(8,128)(2,1)S(1)} %collective-permute-done.4.refs_0_, f32[24,24,128]{2,1,0:T(8,128)S(1)} %get-tuple-element.24.refs_1_.right, f32[1,128]{1,0:T(1,128)S(1)} %get-tuple-element.21.gain.refs_2_, ...), custom_call_target="tpu_custom_call", output_to_operand_aliasing={{}: (4, {})} | custom-call | flops 16777216 | bytes 100000 | tf_op jit(solution)/shard_map/pallas_call | solution.py:146
  9.7 0.0 collective-permute-done.3.passed
  9.8 0.6 %shard_map.78.before = f32[4,12,24,128]{3,2,1,0:T(8,128)S(1)} custom-call(bf16[144,128]{1,0:T(8,128)(2,1)S(1)} %get-tuple-element.25.kept, bf16[144,128]{1,0:T(8,128)(2,1)S(1)} %collective-permute-done.3.passed, f32[24,24,128]{2,1,0:T(8,128)S(1)} %get-tuple-element.24.refs_1_.right, ...), custom_call_target="tpu_custom_call", output_to_operand_aliasing={{}: (5, {})} | custom-call | flops 16777216 | bytes 100000 | tf_op jit(solution)/shard_map/pallas_call | solution.py:146
  10.4 0.5 %collective-permute-done.1.block = bf16[288,128]{1,0:T(8,128)(2,1)S(1)} collective-permute-done((bf16[288,128]{1,0:T(8,128)(2,1)S(1)}, bf16[288,128]{1,0:T(8,128)(2,1)S(1)}, u32[]{:S(2)}, u32[]{:S(2)}) %collective-permute-start.1) | collective-permute-done | bytes 73760 | tf_op jit(solution)/shard_map/ppermute | solution.py:176
  10.9 0.6 %shard_map.79 = (bf16[12,24,128]{2,1,0:T(8,128)(2,1)S(1)}, bf16[12,24,128]{2,1,0:T(8,128)(2,1)S(1)}, bf16[12,24,128]{2,1,0:T(8,128)(2,1)S(1)}, f32[12,24,128]{2,1,0:T(8,128)S(1)}, f32[4,12,24,128]{3,2,1,0:T(8,128)S(1)}) custom-call(bf16[288,128]{1,0:T(8,128)(2,1)S(1)} %collective-permute-done.1.block, ...), custom_call_target="tpu_custom_call", output_to_operand_aliasing={{4}: (4, {})} | custom-call | flops 16777216 | bytes 100000 | tf_op jit(solution)/shard_map/pallas_call | solution.py:146
  11.5 3.7 %collective-permute-start.5 = (bf16[12,24,128]{2,1,0:T(8,128)(2,1)S(1)}, bf16[12,24,128]{2,1,0:T(8,128)(2,1)S(1)}, u32[]{:S(2)}, u32[]{:S(2)}) collective-permute-start(bf16[12,24,128]{2,1,0:T(8,128)(2,1)S(1)} %get-tuple-element.29), channel_id=1, source_target_pairs={{0,24},{1,25},{2,26},{3,27},{4,28},{5,29},{6,30},{7,31},{8,16},{9,... | collective-permute-start | bytes 221192 | tf_op jit(solution)/shard_map/ppermute | solution.py:176
  15.2 0.0 collective-permute-start.6
  15.2 0.8 %collective-permute-start.7 = (bf16[12,24,128]{2,1,0:T(8,128)(2,1)S(1)}, bf16[12,24,128]{2,1,0:T(8,128)(2,1)S(1)}, u32[]{:S(2)}, u32[]{:S(2)}) collective-permute-start(bf16[12,24,128]{2,1,0:T(8,128)(2,1)S(1)} %get-tuple-element.31), channel_id=1, source_target_pairs={{0,16},{1,17},{2,18},{3,19},{4,20},{5,21},{6,22},{7,23},{8,24},{9,... | collective-permute-start | bytes 221192 | tf_op jit(solution)/shard_map/ppermute | solution.py:176
  16.0 0.3 %shard_map.80.refs_4_ = f32[12,24,128]{2,1,0:T(8,128)S(1)} custom-call(bf16[12,24,128]{2,1,0:T(8,128)(2,1)S(1)} %get-tuple-element.20.mine, f32[1,128]{1,0:T(1,128)S(1)} %get-tuple-element.21.gain.refs_2_, bf16[128,128]{1,0:T(8,128)(2,1)S(1)} %get-tuple-element.32.weight), custom_call_target="tpu_custom_call" | custom-call | flops 16777216 | bytes 100000 | tf_op jit(solution)/shard_map/pallas_call | solution.py:146
  16.3 1.6 %collective-permute-done.5.refs_1_ = bf16[12,24,128]{2,1,0:T(8,128)(2,1)S(1)} collective-permute-done((bf16[12,24,128]{2,1,0:T(8,128)(2,1)S(1)}, bf16[12,24,128]{2,1,0:T(8,128)(2,1)S(1)}, u32[]{:S(2)}, u32[]{:S(2)}) %collective-permute-start.5) | collective-permute-done | bytes 73760 | tf_op jit(solution)/shard_map/ppermute | solution.py:176
  17.9 1.6 %collective-permute-done.6.refs_2_ = bf16[12,24,128]{2,1,0:T(8,128)(2,1)S(1)} collective-permute-done((bf16[12,24,128]{2,1,0:T(8,128)(2,1)S(1)}, bf16[12,24,128]{2,1,0:T(8,128)(2,1)S(1)}, u32[]{:S(2)}, u32[]{:S(2)}) %collective-permute-start.6) | collective-permute-done | bytes 73760 | tf_op jit(solution)/shard_map/ppermute | solution.py:176
  19.5 0.9 %collective-permute-done.7.refs_3_ = bf16[12,24,128]{2,1,0:T(8,128)(2,1)S(1)} collective-permute-done((bf16[12,24,128]{2,1,0:T(8,128)(2,1)S(1)}, bf16[12,24,128]{2,1,0:T(8,128)(2,1)S(1)}, u32[]{:S(2)}, u32[]{:S(2)}) %collective-permute-start.7) | collective-permute-done | bytes 73760 | tf_op jit(solution)/shard_map/ppermute | solution.py:176
  20.4 1.0 %shard_map.81 = bf16[12,24,128]{2,1,0:T(8,128)(2,1)} custom-call(f32[12,24,128]{2,1,0:T(8,128)S(1)} %get-tuple-element.28.refs_0_, bf16[12,24,128]{2,1,0:T(8,128)(2,1)S(1)} %collective-permute-done.5.refs_1_, bf16[12,24,128]{2,1,0:T(8,128)(2,1)S(1)} %collective-permute-done.6.refs_2_, bf16[12,24,128]{2,1,0:T(8,128)(2,1)S(1)} %collective-permute-done.7.refs_3_, ...), custom_call_target="tpu_custom_call" | custom-call | flops 16777216 | bytes 100000 | tf_op jit(solution)/shard_map/pallas_call | solution.py:146
  (2 shorter events, 0.1 us)
Async XLA Ops:
  0.0 4.0 %collective-permute-start = (bf16[12,24,128]{2,1,0:T(8,128)(2,1)}, bf16[12,24,128]{2,1,0:T(8,128)(2,1)S(1)}, u32[]{:S(2)}, u32[]{:S(2)}) collective-permute-start(bf16[12,24,128]{2,1,0:T(8,128)(2,1)} %refs_0_.1), channel_id=1, source_target_pairs={{0,4},{1,5},{2,6},{3,7},{4,0},{5,1},{6,2},{7,3},{8,12},{9,13},{10,... | collective-permute-start | bytes 221192 | tf_op jit(solution)/shard_map/ppermute | solution.py:176
  0.5 5.6 %collective-permute-start.2 = (bf16[12,24,128]{2,1,0:T(8,128)(2,1)}, bf16[12,24,128]{2,1,0:T(8,128)(2,1)S(1)}, u32[]{:S(2)}, u32[]{:S(2)}) collective-permute-start(bf16[12,24,128]{2,1,0:T(8,128)(2,1)} %refs_0_.1), channel_id=1, source_target_pairs={{0,1},{1,0},{2,3},{3,2},{4,5},{5,4},{6,7},{7,6},{8,9},{9,8},{10,11... | collective-permute-start | bytes 221192 | tf_op jit(solution)/shard_map/ppermute | solution.py:176
  4.0 5.1 %collective-permute-start.4 = (bf16[288,128]{1,0:T(8,128)(2,1)S(1)}, bf16[288,128]{1,0:T(8,128)(2,1)S(1)}, u32[]{:S(2)}, u32[]{:S(2)}) collective-permute-start(bf16[288,128]{1,0:T(8,128)(2,1)S(1)} %shard_map.74.kept), channel_id=1, source_target_pairs={{0,2},{1,3},{2,0},{3,1},{4,6},{5,7},{6,4},{7,5},{8,10},{9,11},{10,... | collective-permute-start | bytes 221192 | tf_op jit(solution)/shard_map/ppermute | solution.py:176
  5.6 5.3 %collective-permute-start.1 = (bf16[288,128]{1,0:T(8,128)(2,1)S(1)}, bf16[288,128]{1,0:T(8,128)(2,1)S(1)}, u32[]{:S(2)}, u32[]{:S(2)}) collective-permute-start(bf16[288,128]{1,0:T(8,128)(2,1)S(1)} %shard_map.74.kept), channel_id=1, source_target_pairs={{0,3},{1,2},{2,1},{3,0},{4,7},{5,6},{6,5},{7,4},{8,11},{9,10},{10,... | collective-permute-start | bytes 221192 | tf_op jit(solution)/shard_map/ppermute | solution.py:176
  6.2 3.6 %collective-permute-start.3 = (bf16[144,128]{1,0:T(8,128)(2,1)S(1)}, bf16[144,128]{1,0:T(8,128)(2,1)S(1)}, u32[]{:S(2)}, u32[]{:S(2)}) collective-permute-start(bf16[144,128]{1,0:T(8,128)(2,1)S(1)} %get-tuple-element.26), channel_id=1, source_target_pairs={{0,4},{1,5},{2,6},{3,7},{4,0},{5,1},{6,2},{7,3},{8,12},{9,13},{10,... | collective-permute-start | bytes 110600 | tf_op jit(solution)/shard_map/ppermute | solution.py:176
  11.5 6.4 %collective-permute-start.5 = (bf16[12,24,128]{2,1,0:T(8,128)(2,1)S(1)}, bf16[12,24,128]{2,1,0:T(8,128)(2,1)S(1)}, u32[]{:S(2)}, u32[]{:S(2)}) collective-permute-start(bf16[12,24,128]{2,1,0:T(8,128)(2,1)S(1)} %get-tuple-element.29), channel_id=1, source_target_pairs={{0,24},{1,25},{2,26},{3,27},{4,28},{5,29},{6,30},{7,31},{8,16},{9,... | collective-permute-start | bytes 221192 | tf_op jit(solution)/shard_map/ppermute | solution.py:176
  15.2 4.4 %collective-permute-start.6 = (bf16[12,24,128]{2,1,0:T(8,128)(2,1)S(1)}, bf16[12,24,128]{2,1,0:T(8,128)(2,1)S(1)}, u32[]{:S(2)}, u32[]{:S(2)}) collective-permute-start(bf16[12,24,128]{2,1,0:T(8,128)(2,1)S(1)} %get-tuple-element.30), channel_id=1, source_target_pairs={{0,8},{1,9},{2,10},{3,11},{4,12},{5,13},{6,14},{7,15},{8,0},{9,1},... | collective-permute-start | bytes 221192 | tf_op jit(solution)/shard_map/ppermute | solution.py:176
  15.2 5.3 %collective-permute-start.7 = (bf16[12,24,128]{2,1,0:T(8,128)(2,1)S(1)}, bf16[12,24,128]{2,1,0:T(8,128)(2,1)S(1)}, u32[]{:S(2)}, u32[]{:S(2)}) collective-permute-start(bf16[12,24,128]{2,1,0:T(8,128)(2,1)S(1)} %get-tuple-element.31), channel_id=1, source_target_pairs={{0,16},{1,17},{2,18},{3,19},{4,20},{5,21},{6,22},{7,23},{8,24},{9,... | collective-permute-start | bytes 221192 | tf_op jit(solution)/shard_map/ppermute | solution.py:176
where the time goes:
time: 21.5 us; the launch traced here: 21.4 us
  starting transfers between devices  9.49 us (44%)
  waiting for transfers between devices  6.94 us (32%)
  Pallas kernels  4.89 us (23%)
    ppermute x8, starting transfers between devices, swap(): return lax.ppermute(values, axes, pairs)  9.49 us
    ppermute x8, waiting for transfers between devices, swap(): return lax.ppermute(values, axes, pairs)  6.94 us
    pallas_call x9, Pallas kernels, call(): pl.pallas_call(kernel, out_shape=out_shapes, in_specs=[pl.BlockSpec(memor...  4.89 us
  transfers between devices with their start and end apart: 8, of which 6 were waited for; matrix products, arithmetic and copies ran while one was open for 0% of the time, Pallas kernels for 15%

commit v1 on v0

--- a/solution.py
+++ b/solution.py
@@ -9,7 +9,7 @@
 from jax.sharding import PartitionSpec as P
 
 
-EARLY, LATE, ORDER = 1, [2, 3], [3, 1, 2]
+EARLY, LATE, ORDER = 3, [1, 2], [2, 3, 1]
 VMEM = pl.BlockSpec(memory_space=pltpu.VMEM)
 
 
@@ -39,11 +39,11 @@
         flat[pl.ds(at + k * half, half)] = jnp.where(upper, row[half:], row[:half])
 
 
-def pack_kernel(mine, other, out, flat):
+def pack_kernel(mine, other, gain, weight, out, flat):
     upper = core_of() == 1
     cut(mine, upper, flat, 0)
     cut(other, upper, flat, flat.shape[0] // 2)
-    out[...] = flat[...].astype(out.dtype)
+    out[...] = project(flat[...], gain[...], weight[...]).astype(out.dtype)
 
 
 def split_kernel(block, kept, passed, flat):
@@ -91,19 +91,19 @@
             sums[place, base + i] = total
 
 
-def first_kernel(kept, mine, other, gain, left_weight, right_weight, right, sums, left):
+def first_kernel(kept, mine, other, gain, right_weight, right, sums, left):
     rows, columns, width = mine.shape
     for part, block in enumerate((mine, other)):
         flat = project(block[...].reshape(rows * columns, width), gain[...], right_weight[...])
         right[pl.ds(part * rows, rows)] = flat.reshape(rows, columns, -1)
-    left[...] = project(kept[...], gain[...], left_weight[...])
+    left[...] = kept[...].astype(jnp.float32)
     add_block(left, right, sums, lax.axis_index("second"))
 
 
 def middle_kernel(steps, *refs):
-    (right, gain, weight, _, sums, left) = refs[len(steps) :]
+    (right, _, sums, left) = refs[len(steps) :]
     for step, block in zip(steps, refs):
-        left[...] = project(block[...], gain[...], weight[...])
+        left[...] = block[...].astype(jnp.float32)
         add_block(left, right, sums, lax.axis_index("second") ^ step)
 
 
@@ -114,11 +114,11 @@
     add_block(left, right, sums, lax.axis_index("second") ^ step)
 
 
-def last_kernel(step, messages, merge, block, right, gain, weight, before, *refs):
+def last_kernel(step, messages, merge, block, right, before, *refs):
     *outs, sums, left = refs
     first, second = lax.axis_index("first"), lax.axis_index("second")
     chip, core = first // 2, lax.rem(first, 2)
-    left[...] = project(block[...], gain[...], weight[...])
+    left[...] = block[...].astype(jnp.float32)
     add_block(left, right, sums, second ^ step)
     for out, (chips, cores) in zip(outs, messages):
         place = (chip ^ chips) if merge == 1 else 2 * (chip ^ chips) + (core ^ cores)
@@ -177,7 +177,6 @@
 
     lefts = [pltpu.VMEM((depth * half, mix), f32)]
     held = shape((seconds, half, columns, mix), f32)
-    flat = shape((depth * half, width), pair_rows.dtype)
     part = shape((rows * half, width), pair_rows.dtype)
     other = swap(pair_rows, core=1)
     early = swap(pair_rows, block=EARLY)
@@ -197,7 +196,15 @@
         waits=[pltpu.SemaphoreType.DMA((len(arguments),))],
         space=pltpu.HBM,
     )
-    kept = call(pack_kernel, flat, mine, other, scratch=[pltpu.VMEM(flat.shape, f32)])
+    kept = call(
+        pack_kernel,
+        shape((depth * half, mix), jnp.bfloat16),
+        mine,
+        other,
+        in_gain,
+        left_weight,
+        scratch=[pltpu.VMEM((depth * half, width), f32)],
+    )
     late = [s for s in range(1, seconds) if s != EARLY]
     if seconds == 4:
         late = LATE
@@ -210,22 +217,12 @@
         mine,
         other,
         in_gain,
-        left_weight,
         right_weight,
         scratch=lefts,
     )
     factors = (right, in_gain, left_weight)
     near, passed = call(split_kernel, [part, part], early, scratch=[pltpu.VMEM(part.shape, f32)])
     passed = swap(passed, core=1)
-    sums = call(
-        functools.partial(middle_kernel, late[:-1]),
-        held,
-        *blocks,
-        *factors,
-        sums,
-        scratch=lefts,
-        aliases={len(blocks) + 3: 0},
-    )
     sums = call(
         functools.partial(joined_kernel, EARLY),
         held,
@@ -235,6 +232,15 @@
         sums,
         scratch=lefts,
         aliases={5: 0},
+    )
+    sums = call(
+        functools.partial(middle_kernel, late[:-1]),
+        held,
+        *blocks,
+        right,
+        sums,
+        scratch=lefts,
+        aliases={len(blocks) + 1: 0},
     )
     cores = range(merge)
     order = ORDER if chips == 4 else list(range(1, chips))
@@ -244,10 +250,10 @@
         [shape((half, columns, mix), f32 if m == (0, 0) else jnp.bfloat16) for m in messages]
         + [held],
         last,
-        *factors,
+        right,
         sums,
         scratch=lefts,
-        aliases={4: len(messages)},
+        aliases={2: len(messages)},
     )
     gate = call(gate_kernel, shape((rows, columns, wide), f32), mine, in_gain, out_gate)
     arrived = {

time: 21.5 us -> 20.8 us (0.967)
  Pallas kernels: 4.89 us -> 4.51 us
    pallas_call x9, Pallas kernels: 4.89 us -> 4.51 us  [call(): pl.pallas_call(kernel, out_shape=out_shapes, in_specs=[pl.BlockSpec(memor...]
  transfers between devices with their start and end apart: 8 -> 8, of which waited for: 6 -> 7; matrix products, arithmetic and copies ran while one was open for 0% -> 0% of each run, Pallas kernels for 15% -> 16%
where the time goes in v1:
time: 20.8 us; the launch traced here: 20.7 us
  starting transfers between devices  9.32 us (45%)
  waiting for transfers between devices  6.78 us (33%)
  Pallas kernels  4.51 us (22%)
    ppermute x8, starting transfers between devices, swap(): return lax.ppermute(values, axes, pairs)  9.32 us
    ppermute x8, waiting for transfers between devices, swap(): return lax.ppermute(values, axes, pairs)  6.78 us
    pallas_call x9, Pallas kernels, call(): pl.pallas_call(kernel, out_shape=out_shapes, in_specs=[pl.BlockSpec(memor...  4.51 us
  transfers between devices with their start and end apart: 8, of which 7 were waited for; matrix products, arithmetic and copies ran while one was open for 0% of the time, Pallas kernels for 16%

profile of v1, /device:TPU:0, one launch (start us, length us, event | category | flops | bytes accessed | tf_op | source)
XLA Modules:
  0.0 20.7 jit_solution(7145610465701257259)
XLA Ops:
  0.0 0.5 %collective-permute-start = (bf16[12,24,128]{2,1,0:T(8,128)(2,1)}, bf16[12,24,128]{2,1,0:T(8,128)(2,1)S(1)}, u32[]{:S(2)}, u32[]{:S(2)}) collective-permute-start(bf16[12,24,128]{2,1,0:T(8,128)(2,1)} %refs_0_.1), channel_id=1, source_target_pairs={{0,4},{1,5},{2,6},{3,7},{4,0},{5,1},{6,2},{7,3},{8,12},{9,13},{10,... | collective-permute-start | bytes 221192 | tf_op jit(solution)/shard_map/ppermute | solution.py:176
  0.5 3.4 %collective-permute-start.3 = (bf16[12,24,128]{2,1,0:T(8,128)(2,1)}, bf16[12,24,128]{2,1,0:T(8,128)(2,1)S(1)}, u32[]{:S(2)}, u32[]{:S(2)}) collective-permute-start(bf16[12,24,128]{2,1,0:T(8,128)(2,1)} %refs_0_.1), channel_id=1, source_target_pairs={{0,3},{1,2},{2,1},{3,0},{4,7},{5,6},{6,5},{7,4},{8,11},{9,10},{10,... | collective-permute-start | bytes 221192 | tf_op jit(solution)/shard_map/ppermute | solution.py:176
  3.9 1.0 %shard_map.73 = (bf16[12,24,128]{2,1,0:T(8,128)(2,1)S(1)}, f32[1,128]{1,0:T(1,128)S(1)}, bf16[128,128]{1,0:T(8,128)(2,1)S(1)}, bf16[128,128]{1,0:T(8,128)(2,1)S(...) custom-call(bf16[12,24,128]{2,1,0:T(8,128)(2,1)} %refs_0_.1, ...), custom_call_target="tpu_custom_call" | custom-call | flops 16777216 | bytes 100000 | tf_op jit(solution)/shard_map/pallas_call | solution.py:146
  4.9 0.0 collective-permute-done.other
  4.9 0.3 %shard_map.74.kept = bf16[288,128]{1,0:T(8,128)(2,1)S(1)} custom-call(bf16[12,24,128]{2,1,0:T(8,128)(2,1)S(1)} %get-tuple-element.20.mine, bf16[12,24,128]{2,1,0:T(8,128)(2,1)S(1)} %collective-permute-done.other, f32[1,128]{1,0:T(1,128)S(1)} %get-tuple-element.21.gain, bf16[128,128]{1,0:T(8,128)(2,1)S(1)} %get-tuple-element.22.weight), custom_call_target="tpu_custom_call" | custom-call | flops 16777216 | bytes 100000 | tf_op jit(solution)/shard_map/pallas_call | solution.py:146
  5.3 0.6 %collective-permute-start.2 = (bf16[288,128]{1,0:T(8,128)(2,1)S(1)}, bf16[288,128]{1,0:T(8,128)(2,1)S(1)}, u32[]{:S(2)}, u32[]{:S(2)}) collective-permute-start(bf16[288,128]{1,0:T(8,128)(2,1)S(1)} %shard_map.74.kept), channel_id=1, source_target_pairs={{0,1},{1,0},{2,3},{3,2},{4,5},{5,4},{6,7},{7,6},{8,9},{9,8},{10,11... | collective-permute-start | bytes 221192 | tf_op jit(solution)/shard_map/ppermute | solution.py:176
  5.9 0.5 %collective-permute-start.1 = (bf16[288,128]{1,0:T(8,128)(2,1)S(1)}, bf16[288,128]{1,0:T(8,128)(2,1)S(1)}, u32[]{:S(2)}, u32[]{:S(2)}) collective-permute-start(bf16[288,128]{1,0:T(8,128)(2,1)S(1)} %shard_map.74.kept), channel_id=1, source_target_pairs={{0,2},{1,3},{2,0},{3,1},{4,6},{5,7},{6,4},{7,5},{8,10},{9,11},{10,... | collective-permute-start | bytes 221192 | tf_op jit(solution)/shard_map/ppermute | solution.py:176
  6.4 0.7 %collective-permute-done.3.block = bf16[12,24,128]{2,1,0:T(8,128)(2,1)S(1)} collective-permute-done((bf16[12,24,128]{2,1,0:T(8,128)(2,1)}, bf16[12,24,128]{2,1,0:T(8,128)(2,1)S(1)}, u32[]{:S(2)}, u32[]{:S(2)}) %collective-permute-start.3) | collective-permute-done | bytes 73760 | tf_op jit(solution)/shard_map/ppermute | solution.py:176
  7.1 0.1 collective-permute-start.4
  7.2 0.6 %shard_map.75 = (f32[24,24,128]{2,1,0:T(8,128)S(1)}, f32[4,12,24,128]{3,2,1,0:T(8,128)S(1)}) custom-call(bf16[288,128]{1,0:T(8,128)(2,1)S(1)} %shard_map.74.kept, bf16[12,24,128]{2,1,0:T(8,128)(2,1)S(1)} %get-tuple-element.20.mine, bf16[12,24,128]{2,1,0:T(8,128)(2,1)S(1)} %collective-permute-done.other, f32[1,128]{1,0:T(1,128)S(1)} %get-tuple-element.21.gain, ...), custom_call_target="tpu_custom_call" | custom-call | flops 16777216 | bytes 100000 | tf_op jit(solution)/shard_map/pallas_call | solution.py:146
  7.8 0.6 %collective-permute-done.4.passed = bf16[144,128]{1,0:T(8,128)(2,1)S(1)} collective-permute-done((bf16[144,128]{1,0:T(8,128)(2,1)S(1)}, bf16[144,128]{1,0:T(8,128)(2,1)S(1)}, u32[]{:S(2)}, u32[]{:S(2)}) %collective-permute-start.4) | collective-permute-done | bytes 36896 | tf_op jit(solution)/shard_map/ppermute | solution.py:176
  8.4 0.6 %shard_map.77.refs_2_ = f32[4,12,24,128]{3,2,1,0:T(8,128)S(1)} custom-call(bf16[144,128]{1,0:T(8,128)(2,1)S(1)} %get-tuple-element.25.kept, bf16[144,128]{1,0:T(8,128)(2,1)S(1)} %collective-permute-done.4.passed, f32[24,24,128]{2,1,0:T(8,128)S(1)} %get-tuple-element.24.right.refs_1_, ...), custom_call_target="tpu_custom_call", output_to_operand_aliasing={{}: (5, {})} | custom-call | flops 16777216 | bytes 100000 | tf_op jit(solution)/shard_map/pallas_call | solution.py:146
  9.0 0.7 %collective-permute-done.2.refs_0_ = bf16[288,128]{1,0:T(8,128)(2,1)S(1)} collective-permute-done((bf16[288,128]{1,0:T(8,128)(2,1)S(1)}, bf16[288,128]{1,0:T(8,128)(2,1)S(1)}, u32[]{:S(2)}, u32[]{:S(2)}) %collective-permute-start.2) | collective-permute-done | bytes 73760 | tf_op jit(solution)/shard_map/ppermute | solution.py:176
  9.8 0.3 %shard_map.78.before = f32[4,12,24,128]{3,2,1,0:T(8,128)S(1)} custom-call(bf16[288,128]{1,0:T(8,128)(2,1)S(1)} %collective-permute-done.2.refs_0_, f32[24,24,128]{2,1,0:T(8,128)S(1)} %get-tuple-element.24.right.refs_1_, f32[4,12,24,128]{3,2,1,0:T(8,128)S(1)} %shard_map.77.refs_2_), custom_call_target="tpu_custom_call", output_to_operand_aliasing={{}: (2, {})} | custom-call | flops 16777216 | bytes 100000 | tf_op jit(solution)/shard_map/pallas_call | solution.py:146
  10.0 0.2 collective-permute-done.1.block
  10.2 0.3 %shard_map.79 = (bf16[12,24,128]{2,1,0:T(8,128)(2,1)S(1)}, bf16[12,24,128]{2,1,0:T(8,128)(2,1)S(1)}, bf16[12,24,128]{2,1,0:T(8,128)(2,1)S(1)}, f32[12,24,128]{2,1,0:T(8,128)S(1)}, f32[4,12,24,128]{3,2,1,0:T(8,128)S(1)}) custom-call(bf16[288,128]{1,0:T(8,128)(2,1)S(1)} %collective-permute-done.1.block, ...), custom_call_target="tpu_custom_call", output_to_operand_aliasing={{4}: (2, {})} | custom-call | flops 16777216 | bytes 100000 | tf_op jit(solution)/shard_map/pallas_call | solution.py:146
  10.6 2.7 %collective-permute-start.5 = (bf16[12,24,128]{2,1,0:T(8,128)(2,1)S(1)}, bf16[12,24,128]{2,1,0:T(8,128)(2,1)S(1)}, u32[]{:S(2)}, u32[]{:S(2)}) collective-permute-start(bf16[12,24,128]{2,1,0:T(8,128)(2,1)S(1)} %get-tuple-element.29), channel_id=1, source_target_pairs={{0,16},{1,17},{2,18},{3,19},{4,20},{5,21},{6,22},{7,23},{8,24},{9,... | collective-permute-start | bytes 221192 | tf_op jit(solution)/shard_map/ppermute | solution.py:176
  13.2 1.3 %collective-permute-start.6 = (bf16[12,24,128]{2,1,0:T(8,128)(2,1)S(1)}, bf16[12,24,128]{2,1,0:T(8,128)(2,1)S(1)}, u32[]{:S(2)}, u32[]{:S(2)}) collective-permute-start(bf16[12,24,128]{2,1,0:T(8,128)(2,1)S(1)} %get-tuple-element.30), channel_id=1, source_target_pairs={{0,24},{1,25},{2,26},{3,27},{4,28},{5,29},{6,30},{7,31},{8,16},{9,... | collective-permute-start | bytes 221192 | tf_op jit(solution)/shard_map/ppermute | solution.py:176
  14.6 0.2 %collective-permute-start.7 = (bf16[12,24,128]{2,1,0:T(8,128)(2,1)S(1)}, bf16[12,24,128]{2,1,0:T(8,128)(2,1)S(1)}, u32[]{:S(2)}, u32[]{:S(2)}) collective-permute-start(bf16[12,24,128]{2,1,0:T(8,128)(2,1)S(1)} %get-tuple-element.31), channel_id=1, source_target_pairs={{0,8},{1,9},{2,10},{3,11},{4,12},{5,13},{6,14},{7,15},{8,0},{9,1},... | collective-permute-start | bytes 221192 | tf_op jit(solution)/shard_map/ppermute | solution.py:176
  14.8 0.3 %shard_map.80.refs_4_ = f32[12,24,128]{2,1,0:T(8,128)S(1)} custom-call(bf16[12,24,128]{2,1,0:T(8,128)(2,1)S(1)} %get-tuple-element.20.mine, f32[1,128]{1,0:T(1,128)S(1)} %get-tuple-element.21.gain, bf16[128,128]{1,0:T(8,128)(2,1)S(1)} %get-tuple-element.32.weight), custom_call_target="tpu_custom_call" | custom-call | flops 16777216 | bytes 100000 | tf_op jit(solution)/shard_map/pallas_call | solution.py:146
  15.1 2.8 %collective-permute-done.5.refs_1_ = bf16[12,24,128]{2,1,0:T(8,128)(2,1)S(1)} collective-permute-done((bf16[12,24,128]{2,1,0:T(8,128)(2,1)S(1)}, bf16[12,24,128]{2,1,0:T(8,128)(2,1)S(1)}, u32[]{:S(2)}, u32[]{:S(2)}) %collective-permute-start.5) | collective-permute-done | bytes 73760 | tf_op jit(solution)/shard_map/ppermute | solution.py:176
  17.9 1.6 %collective-permute-done.6.refs_2_ = bf16[12,24,128]{2,1,0:T(8,128)(2,1)S(1)} collective-permute-done((bf16[12,24,128]{2,1,0:T(8,128)(2,1)S(1)}, bf16[12,24,128]{2,1,0:T(8,128)(2,1)S(1)}, u32[]{:S(2)}, u32[]{:S(2)}) %collective-permute-start.6) | collective-permute-done | bytes 73760 | tf_op jit(solution)/shard_map/ppermute | solution.py:176
  19.5 0.2 %collective-permute-done.7.refs_3_ = bf16[12,24,128]{2,1,0:T(8,128)(2,1)S(1)} collective-permute-done((bf16[12,24,128]{2,1,0:T(8,128)(2,1)S(1)}, bf16[12,24,128]{2,1,0:T(8,128)(2,1)S(1)}, u32[]{:S(2)}, u32[]{:S(2)}) %collective-permute-start.7) | collective-permute-done | bytes 73760 | tf_op jit(solution)/shard_map/ppermute | solution.py:176
  19.7 1.0 %shard_map.81 = bf16[12,24,128]{2,1,0:T(8,128)(2,1)} custom-call(f32[12,24,128]{2,1,0:T(8,128)S(1)} %get-tuple-element.28.refs_0_, bf16[12,24,128]{2,1,0:T(8,128)(2,1)S(1)} %collective-permute-done.5.refs_1_, bf16[12,24,128]{2,1,0:T(8,128)(2,1)S(1)} %collective-permute-done.6.refs_2_, bf16[12,24,128]{2,1,0:T(8,128)(2,1)S(1)} %collective-permute-done.7.refs_3_, ...), custom_call_target="tpu_custom_call" | custom-call | flops 16777216 | bytes 100000 | tf_op jit(solution)/shard_map/pallas_call | solution.py:146
  (1 shorter events, 0.0 us)
Async XLA Ops:
  0.0 4.9 %collective-permute-start = (bf16[12,24,128]{2,1,0:T(8,128)(2,1)}, bf16[12,24,128]{2,1,0:T(8,128)(2,1)S(1)}, u32[]{:S(2)}, u32[]{:S(2)}) collective-permute-start(bf16[12,24,128]{2,1,0:T(8,128)(2,1)} %refs_0_.1), channel_id=1, source_target_pairs={{0,4},{1,5},{2,6},{3,7},{4,0},{5,1},{6,2},{7,3},{8,12},{9,13},{10,... | collective-permute-start | bytes 221192 | tf_op jit(solution)/shard_map/ppermute | solution.py:176
  0.5 6.6 %collective-permute-start.3 = (bf16[12,24,128]{2,1,0:T(8,128)(2,1)}, bf16[12,24,128]{2,1,0:T(8,128)(2,1)S(1)}, u32[]{:S(2)}, u32[]{:S(2)}) collective-permute-start(bf16[12,24,128]{2,1,0:T(8,128)(2,1)} %refs_0_.1), channel_id=1, source_target_pairs={{0,3},{1,2},{2,1},{3,0},{4,7},{5,6},{6,5},{7,4},{8,11},{9,10},{10,... | collective-permute-start | bytes 221192 | tf_op jit(solution)/shard_map/ppermute | solution.py:176
  5.3 4.5 %collective-permute-start.2 = (bf16[288,128]{1,0:T(8,128)(2,1)S(1)}, bf16[288,128]{1,0:T(8,128)(2,1)S(1)}, u32[]{:S(2)}, u32[]{:S(2)}) collective-permute-start(bf16[288,128]{1,0:T(8,128)(2,1)S(1)} %shard_map.74.kept), channel_id=1, source_target_pairs={{0,1},{1,0},{2,3},{3,2},{4,5},{5,4},{6,7},{7,6},{8,9},{9,8},{10,11... | collective-permute-start | bytes 221192 | tf_op jit(solution)/shard_map/ppermute | solution.py:176
  5.9 4.4 %collective-permute-start.1 = (bf16[288,128]{1,0:T(8,128)(2,1)S(1)}, bf16[288,128]{1,0:T(8,128)(2,1)S(1)}, u32[]{:S(2)}, u32[]{:S(2)}) collective-permute-start(bf16[288,128]{1,0:T(8,128)(2,1)S(1)} %shard_map.74.kept), channel_id=1, source_target_pairs={{0,2},{1,3},{2,0},{3,1},{4,6},{5,7},{6,4},{7,5},{8,10},{9,11},{10,... | collective-permute-start | bytes 221192 | tf_op jit(solution)/shard_map/ppermute | solution.py:176
  7.1 1.3 %collective-permute-start.4 = (bf16[144,128]{1,0:T(8,128)(2,1)S(1)}, bf16[144,128]{1,0:T(8,128)(2,1)S(1)}, u32[]{:S(2)}, u32[]{:S(2)}) collective-permute-start(bf16[144,128]{1,0:T(8,128)(2,1)S(1)} %get-tuple-element.26), channel_id=1, source_target_pairs={{0,4},{1,5},{2,6},{3,7},{4,0},{5,1},{6,2},{7,3},{8,12},{9,13},{10,... | collective-permute-start | bytes 110600 | tf_op jit(solution)/shard_map/ppermute | solution.py:176
  10.6 7.3 %collective-permute-start.5 = (bf16[12,24,128]{2,1,0:T(8,128)(2,1)S(1)}, bf16[12,24,128]{2,1,0:T(8,128)(2,1)S(1)}, u32[]{:S(2)}, u32[]{:S(2)}) collective-permute-start(bf16[12,24,128]{2,1,0:T(8,128)(2,1)S(1)} %get-tuple-element.29), channel_id=1, source_target_pairs={{0,16},{1,17},{2,18},{3,19},{4,20},{5,21},{6,22},{7,23},{8,24},{9,... | collective-permute-start | bytes 221192 | tf_op jit(solution)/shard_map/ppermute | solution.py:176
  13.2 6.3 %collective-permute-start.6 = (bf16[12,24,128]{2,1,0:T(8,128)(2,1)S(1)}, bf16[12,24,128]{2,1,0:T(8,128)(2,1)S(1)}, u32[]{:S(2)}, u32[]{:S(2)}) collective-permute-start(bf16[12,24,128]{2,1,0:T(8,128)(2,1)S(1)} %get-tuple-element.30), channel_id=1, source_target_pairs={{0,24},{1,25},{2,26},{3,27},{4,28},{5,29},{6,30},{7,31},{8,16},{9,... | collective-permute-start | bytes 221192 | tf_op jit(solution)/shard_map/ppermute | solution.py:176
  14.6 5.1 %collective-permute-start.7 = (bf16[12,24,128]{2,1,0:T(8,128)(2,1)S(1)}, bf16[12,24,128]{2,1,0:T(8,128)(2,1)S(1)}, u32[]{:S(2)}, u32[]{:S(2)}) collective-permute-start(bf16[12,24,128]{2,1,0:T(8,128)(2,1)S(1)} %get-tuple-element.31), channel_id=1, source_target_pairs={{0,8},{1,9},{2,10},{3,11},{4,12},{5,13},{6,14},{7,15},{8,0},{9,1},... | collective-permute-start | bytes 221192 | tf_op jit(solution)/shard_map/ppermute | solution.py:176

commit v2 on v1

--- a/solution.py
+++ b/solution.py
@@ -9,7 +9,6 @@
 from jax.sharding import PartitionSpec as P
 
 
-EARLY, LATE, ORDER = 3, [1, 2], [2, 3, 1]
 VMEM = pl.BlockSpec(memory_space=pltpu.VMEM)
 
 
@@ -72,20 +71,22 @@
     out[...] = jax.nn.sigmoid(dot(ready, weight[...])).reshape(rows, columns, -1)
 
 
-def add_block(left, right, sums, place):
-    depth, columns, width = right.shape
-    half = left.shape[0] // depth
+def add_block(left, right, sums, place, start=0, more=False):
+    _, half, columns, width = sums.shape
+    depth = left.shape[0] // half
     group = max(g for g in range(1, half + 1) if half % g == 0 and g * columns <= 288)
     for base in range(0, half, group):
 
         def step(k, totals):
-            line = right[k]
+            line = right[start + k]
             return tuple(
                 total + left[pl.ds(k * half + base + i, 1)] * line
                 for i, total in enumerate(totals)
             )
 
         totals = (jnp.zeros((columns, width), jnp.float32),) * group
+        if more:
+            totals = tuple(sums[place, base + i] for i in range(group))
         totals = lax.fori_loop(0, depth, step, totals, unroll=6)
         for i, total in enumerate(totals):
             sums[place, base + i] = total
@@ -107,11 +108,10 @@
         add_block(left, right, sums, lax.axis_index("second") ^ step)
 
 
-def joined_kernel(step, kept, passed, right, gain, weight, _, sums, left):
-    rows = kept.shape[0]
-    for part, block in enumerate((kept, passed)):
-        left[pl.ds(part * rows, rows)] = project(block[...], gain[...], weight[...])
-    add_block(left, right, sums, lax.axis_index("second") ^ step)
+def part_kernel(step, more, block, right, gain, weight, _, sums, left):
+    left[...] = project(block[...], gain[...], weight[...])
+    start = right.shape[0] // 2 if more else 0
+    add_block(left, right, sums, lax.axis_index("second") ^ step, start, more)
 
 
 def last_kernel(step, messages, merge, block, right, before, *refs):
@@ -120,8 +120,11 @@
     chip, core = first // 2, lax.rem(first, 2)
     left[...] = block[...].astype(jnp.float32)
     add_block(left, right, sums, second ^ step)
-    for out, (chips, cores) in zip(outs, messages):
-        place = (chip ^ chips) if merge == 1 else 2 * (chip ^ chips) + (core ^ cores)
+    for out, (targets, cores) in zip(outs, messages):
+        place = jnp.int32(0)
+        for z, target in enumerate(targets):
+            place = jnp.where(chip == z, target, place)
+        place = place if merge == 1 else 2 * place + (core ^ cores)
         out[...] = sums[place].astype(out.dtype)
 
 
@@ -167,9 +170,14 @@
     axes = ("first", "second")
     shape, f32 = jax.ShapeDtypeStruct, jnp.float32
 
-    def swap(values, chip=0, core=0, block=0):
+    ring = [0, *range(1, chips, 2), *range(2, chips, 2)[::-1]]
+    targets = [
+        [ring[(ring.index(z) + step) % chips] for z in range(chips)] for step in range(chips)
+    ]
+
+    def swap(values, step=0, core=0, block=0):
         pairs = [
-            (a * seconds + b, (a ^ (2 * chip + core)) * seconds + (b ^ block))
+            (a * seconds + b, (2 * targets[step][a // 2] + (a % 2 ^ core)) * seconds + (b ^ block))
             for a in range(firsts)
             for b in range(seconds)
         ]
@@ -179,7 +187,7 @@
     held = shape((seconds, half, columns, mix), f32)
     part = shape((rows * half, width), pair_rows.dtype)
     other = swap(pair_rows, core=1)
-    early = swap(pair_rows, block=EARLY)
+    early = swap(pair_rows, block=seconds - 1)
     arguments = (
         pair_rows,
         in_gain,
@@ -205,9 +213,7 @@
         left_weight,
         scratch=[pltpu.VMEM((depth * half, width), f32)],
     )
-    late = [s for s in range(1, seconds) if s != EARLY]
-    if seconds == 4:
-        late = LATE
+    late = list(range(1, seconds - 1))
     blocks = [swap(kept, block=s) for s in late[:-1]]
     last = swap(kept, block=late[-1])
     right, sums = call(
@@ -223,16 +229,16 @@
     factors = (right, in_gain, left_weight)
     near, passed = call(split_kernel, [part, part], early, scratch=[pltpu.VMEM(part.shape, f32)])
     passed = swap(passed, core=1)
-    sums = call(
-        functools.partial(joined_kernel, EARLY),
-        held,
-        near,
-        passed,
-        *factors,
-        sums,
-        scratch=lefts,
-        aliases={5: 0},
-    )
+    for block, more in ((near, False), (passed, True)):
+        sums = call(
+            functools.partial(part_kernel, seconds - 1, more),
+            held,
+            block,
+            *factors,
+            sums,
+            scratch=[pltpu.VMEM((rows * half, mix), f32)],
+            aliases={4: 0},
+        )
     sums = call(
         functools.partial(middle_kernel, late[:-1]),
         held,
@@ -243,10 +249,11 @@
         aliases={len(blocks) + 1: 0},
     )
     cores = range(merge)
-    order = ORDER if chips == 4 else list(range(1, chips))
-    messages = [(t, c) for t in order + [0] for c in reversed(cores)]
+    messages = [(t, c) for t in [*range(1, chips), 0] for c in reversed(cores)]
     *outgoing, _ = call(
-        functools.partial(last_kernel, late[-1], messages, merge),
+        functools.partial(
+            last_kernel, late[-1], [(targets[t], c) for t, c in messages], merge
+        ),
         [shape((half, columns, mix), f32 if m == (0, 0) else jnp.bfloat16) for m in messages]
         + [held],
         last,
@@ -257,10 +264,10 @@
     )
     gate = call(gate_kernel, shape((rows, columns, wide), f32), mine, in_gain, out_gate)
     arrived = {
-        (t, c): sent if (t, c) == (0, 0) else swap(sent, chip=t, core=c)
+        (t, c): sent if (t, c) == (0, 0) else swap(sent, step=t, core=c)
         for (t, c), sent in zip(messages, outgoing)
     }
-    parts = [arrived[t, c] for c in cores for t in [0] + order]
+    parts = [arrived[t, c] for c in cores for t in range(chips)]
     return call(
         functools.partial(final_kernel, merge, chips, (rows * firsts) ** -0.5),
         shape((rows, columns, wide), jnp.bfloat16),

time: 20.8 us -> 20.7 us (level)
  waiting for transfers between devices: 6.78 us -> 4.91 us
  starting transfers between devices: 9.32 us -> 10.8 us
  Pallas kernels: 4.51 us -> 4.79 us
    ppermute x8, waiting for transfers between devices: 6.78 us -> 4.91 us  [swap(): return lax.ppermute(values, axes, pairs)]
    ppermute x8, starting transfers between devices: 9.32 us -> 10.8 us  [swap(): return lax.ppermute(values, axes, pairs)]
    pallas_call x9 -> x10, Pallas kernels: 4.51 us -> 4.79 us  [call(): pl.pallas_call(kernel, out_shape=out_shapes, in_specs=[pl.BlockSpec(memor...]
  transfers between devices with their start and end apart: 8 -> 8, of which waited for: 7 -> 6; matrix products, arithmetic and copies ran while one was open for 0% -> 0% of each run, Pallas kernels for 16% -> 17%
where the time goes in v2:
time: 20.7 us; the launch traced here: 20.6 us
  starting transfers between devices  10.8 us (52%)
  waiting for transfers between devices  4.91 us (24%)
  Pallas kernels  4.79 us (23%)
    ppermute x8, starting transfers between devices, swap(): return lax.ppermute(values, axes, pairs)  10.8 us
    ppermute x8, waiting for transfers between devices, swap(): return lax.ppermute(values, axes, pairs)  4.91 us
    pallas_call x10, Pallas kernels, call(): pl.pallas_call(kernel, out_shape=out_shapes, in_specs=[pl.BlockSpec(memor...  4.79 us
  transfers between devices with their start and end apart: 8, of which 6 were waited for; matrix products, arithmetic and copies ran while one was open for 0% of the time, Pallas kernels for 17%

profile of v2, /device:TPU:0, one launch (start us, length us, event | category | flops | bytes accessed | tf_op | source)
XLA Modules:
  0.0 20.6 jit_solution(5896078759168651516)
XLA Ops:
  0.0 0.5 %collective-permute-start = (bf16[12,24,128]{2,1,0:T(8,128)(2,1)}, bf16[12,24,128]{2,1,0:T(8,128)(2,1)S(1)}, u32[]{:S(2)}, u32[]{:S(2)}) collective-permute-start(bf16[12,24,128]{2,1,0:T(8,128)(2,1)} %refs_0_.1), channel_id=1, source_target_pairs={{0,4},{1,5},{2,6},{3,7},{4,0},{5,1},{6,2},{7,3},{8,12},{9,13},{10,... | collective-permute-start | bytes 221192 | tf_op jit(solution)/shard_map/ppermute | solution.py:184
  0.5 3.4 %collective-permute-start.3 = (bf16[12,24,128]{2,1,0:T(8,128)(2,1)}, bf16[12,24,128]{2,1,0:T(8,128)(2,1)S(1)}, u32[]{:S(2)}, u32[]{:S(2)}) collective-permute-start(bf16[12,24,128]{2,1,0:T(8,128)(2,1)} %refs_0_.1), channel_id=1, source_target_pairs={{0,3},{1,2},{2,1},{3,0},{4,7},{5,6},{6,5},{7,4},{8,11},{9,10},{10,... | collective-permute-start | bytes 221192 | tf_op jit(solution)/shard_map/ppermute | solution.py:184
  3.9 1.0 %shard_map.73 = (bf16[12,24,128]{2,1,0:T(8,128)(2,1)S(1)}, f32[1,128]{1,0:T(1,128)S(1)}, bf16[128,128]{1,0:T(8,128)(2,1)S(1)}, bf16[128,128]{1,0:T(8,128)(2,1)S(...) custom-call(bf16[12,24,128]{2,1,0:T(8,128)(2,1)} %refs_0_.1, ...), custom_call_target="tpu_custom_call" | custom-call | flops 16777216 | bytes 100000 | tf_op jit(solution)/shard_map/pallas_call | solution.py:149
  4.9 0.0 collective-permute-done.other
  4.9 0.3 %shard_map.74.kept = bf16[288,128]{1,0:T(8,128)(2,1)S(1)} custom-call(bf16[12,24,128]{2,1,0:T(8,128)(2,1)S(1)} %get-tuple-element.20.mine, bf16[12,24,128]{2,1,0:T(8,128)(2,1)S(1)} %collective-permute-done.other, f32[1,128]{1,0:T(1,128)S(1)} %get-tuple-element.21.gain, bf16[128,128]{1,0:T(8,128)(2,1)S(1)} %get-tuple-element.22.weight), custom_call_target="tpu_custom_call" | custom-call | flops 16777216 | bytes 100000 | tf_op jit(solution)/shard_map/pallas_call | solution.py:149
  5.3 0.6 %collective-permute-start.2 = (bf16[288,128]{1,0:T(8,128)(2,1)S(1)}, bf16[288,128]{1,0:T(8,128)(2,1)S(1)}, u32[]{:S(2)}, u32[]{:S(2)}) collective-permute-start(bf16[288,128]{1,0:T(8,128)(2,1)S(1)} %shard_map.74.kept), channel_id=1, source_target_pairs={{0,1},{1,0},{2,3},{3,2},{4,5},{5,4},{6,7},{7,6},{8,9},{9,8},{10,11... | collective-permute-start | bytes 221192 | tf_op jit(solution)/shard_map/ppermute | solution.py:184
  5.9 0.5 %collective-permute-start.1 = (bf16[288,128]{1,0:T(8,128)(2,1)S(1)}, bf16[288,128]{1,0:T(8,128)(2,1)S(1)}, u32[]{:S(2)}, u32[]{:S(2)}) collective-permute-start(bf16[288,128]{1,0:T(8,128)(2,1)S(1)} %shard_map.74.kept), channel_id=1, source_target_pairs={{0,2},{1,3},{2,0},{3,1},{4,6},{5,7},{6,4},{7,5},{8,10},{9,11},{10,... | collective-permute-start | bytes 221192 | tf_op jit(solution)/shard_map/ppermute | solution.py:184
  6.4 0.7 %collective-permute-done.3.block = bf16[12,24,128]{2,1,0:T(8,128)(2,1)S(1)} collective-permute-done((bf16[12,24,128]{2,1,0:T(8,128)(2,1)}, bf16[12,24,128]{2,1,0:T(8,128)(2,1)S(1)}, u32[]{:S(2)}, u32[]{:S(2)}) %collective-permute-start.3) | collective-permute-done | bytes 73760 | tf_op jit(solution)/shard_map/ppermute | solution.py:184
  7.1 0.1 collective-permute-start.4
  7.2 0.6 %shard_map.75 = (f32[24,24,128]{2,1,0:T(8,128)S(1)}, f32[4,12,24,128]{3,2,1,0:T(8,128)S(1)}) custom-call(bf16[288,128]{1,0:T(8,128)(2,1)S(1)} %shard_map.74.kept, bf16[12,24,128]{2,1,0:T(8,128)(2,1)S(1)} %get-tuple-element.20.mine, bf16[12,24,128]{2,1,0:T(8,128)(2,1)S(1)} %collective-permute-done.other, f32[1,128]{1,0:T(1,128)S(1)} %get-tuple-element.21.gain, ...), custom_call_target="tpu_custom_call" | custom-call | flops 16777216 | bytes 100000 | tf_op jit(solution)/shard_map/pallas_call | solution.py:149
  7.8 0.5 %shard_map.77._ = f32[4,12,24,128]{3,2,1,0:T(8,128)S(1)} custom-call(bf16[144,128]{1,0:T(8,128)(2,1)S(1)} %get-tuple-element.26.block, f32[24,24,128]{2,1,0:T(8,128)S(1)} %get-tuple-element.24.right.refs_1_, f32[1,128]{1,0:T(1,128)S(1)} %get-tuple-element.21.gain, bf16[128,128]{1,0:T(8,128)(2,1)S(1)} %get-tuple-element.22.weight, ...), custom_call_target="tpu_custom_call", output_to_operand_aliasing={{}: (4, {})} | custom-call | flops 16777216 | bytes 100000 | tf_op jit(solution)/shard_map/pallas_call | solution.py:149
  8.3 0.1 collective-permute-done.4.block
  8.4 0.4 %shard_map.78.refs_2_ = f32[4,12,24,128]{3,2,1,0:T(8,128)S(1)} custom-call(bf16[144,128]{1,0:T(8,128)(2,1)S(1)} %collective-permute-done.4.block, f32[24,24,128]{2,1,0:T(8,128)S(1)} %get-tuple-element.24.right.refs_1_, f32[1,128]{1,0:T(1,128)S(1)} %get-tuple-element.21.gain, ...), custom_call_target="tpu_custom_call", output_to_operand_aliasing={{}: (4, {})} | custom-call | flops 16777216 | bytes 100000 | tf_op jit(solution)/shard_map/pallas_call | solution.py:149
  8.8 0.9 %collective-permute-done.2.refs_0_ = bf16[288,128]{1,0:T(8,128)(2,1)S(1)} collective-permute-done((bf16[288,128]{1,0:T(8,128)(2,1)S(1)}, bf16[288,128]{1,0:T(8,128)(2,1)S(1)}, u32[]{:S(2)}, u32[]{:S(2)}) %collective-permute-start.2) | collective-permute-done | bytes 73760 | tf_op jit(solution)/shard_map/ppermute | solution.py:184
  9.8 0.3 %shard_map.79.before = f32[4,12,24,128]{3,2,1,0:T(8,128)S(1)} custom-call(bf16[288,128]{1,0:T(8,128)(2,1)S(1)} %collective-permute-done.2.refs_0_, f32[24,24,128]{2,1,0:T(8,128)S(1)} %get-tuple-element.24.right.refs_1_, f32[4,12,24,128]{3,2,1,0:T(8,128)S(1)} %shard_map.78.refs_2_), custom_call_target="tpu_custom_call", output_to_operand_aliasing={{}: (2, {})} | custom-call | flops 16777216 | bytes 100000 | tf_op jit(solution)/shard_map/pallas_call | solution.py:149
  10.0 0.2 collective-permute-done.1.block
  10.2 0.3 %shard_map.80 = (bf16[12,24,128]{2,1,0:T(8,128)(2,1)S(1)}, bf16[12,24,128]{2,1,0:T(8,128)(2,1)S(1)}, bf16[12,24,128]{2,1,0:T(8,128)(2,1)S(1)}, f32[12,24,128]{2,1,0:T(8,128)S(1)}, f32[4,12,24,128]{3,2,1,0:T(8,128)S(1)}) custom-call(bf16[288,128]{1,0:T(8,128)(2,1)S(1)} %collective-permute-done.1.block, ...), custom_call_target="tpu_custom_call", output_to_operand_aliasing={{4}: (2, {})} | custom-call | flops 16777216 | bytes 100000 | tf_op jit(solution)/shard_map/pallas_call | solution.py:149
  10.6 1.6 %collective-permute-start.5 = (bf16[12,24,128]{2,1,0:T(8,128)(2,1)S(1)}, bf16[12,24,128]{2,1,0:T(8,128)(2,1)S(1)}, u32[]{:S(2)}, u32[]{:S(2)}) collective-permute-start(bf16[12,24,128]{2,1,0:T(8,128)(2,1)S(1)} %get-tuple-element.29), channel_id=1, source_target_pairs={{0,8},{1,9},{2,10},{3,11},{4,12},{5,13},{6,14},{7,15},{8,24},{9,25... | collective-permute-start | bytes 221192 | tf_op jit(solution)/shard_map/ppermute | solution.py:184
  12.2 2.5 %collective-permute-start.6 = (bf16[12,24,128]{2,1,0:T(8,128)(2,1)S(1)}, bf16[12,24,128]{2,1,0:T(8,128)(2,1)S(1)}, u32[]{:S(2)}, u32[]{:S(2)}) collective-permute-start(bf16[12,24,128]{2,1,0:T(8,128)(2,1)S(1)} %get-tuple-element.30), channel_id=1, source_target_pairs={{0,24},{1,25},{2,26},{3,27},{4,28},{5,29},{6,30},{7,31},{8,16},{9,... | collective-permute-start | bytes 221192 | tf_op jit(solution)/shard_map/ppermute | solution.py:184
  14.7 1.6 %collective-permute-start.7 = (bf16[12,24,128]{2,1,0:T(8,128)(2,1)S(1)}, bf16[12,24,128]{2,1,0:T(8,128)(2,1)S(1)}, u32[]{:S(2)}, u32[]{:S(2)}) collective-permute-start(bf16[12,24,128]{2,1,0:T(8,128)(2,1)S(1)} %get-tuple-element.31), channel_id=1, source_target_pairs={{0,16},{1,17},{2,18},{3,19},{4,20},{5,21},{6,22},{7,23},{8,0},{9,1... | collective-permute-start | bytes 221192 | tf_op jit(solution)/shard_map/ppermute | solution.py:184
  16.2 0.3 %shard_map.81.refs_4_ = f32[12,24,128]{2,1,0:T(8,128)S(1)} custom-call(bf16[12,24,128]{2,1,0:T(8,128)(2,1)S(1)} %get-tuple-element.20.mine, f32[1,128]{1,0:T(1,128)S(1)} %get-tuple-element.21.gain, bf16[128,128]{1,0:T(8,128)(2,1)S(1)} %get-tuple-element.32.weight), custom_call_target="tpu_custom_call" | custom-call | flops 16777216 | bytes 100000 | tf_op jit(solution)/shard_map/pallas_call | solution.py:149
  16.6 0.0 collective-permute-done.5.refs_1_
  16.6 2.5 %collective-permute-done.6.refs_2_ = bf16[12,24,128]{2,1,0:T(8,128)(2,1)S(1)} collective-permute-done((bf16[12,24,128]{2,1,0:T(8,128)(2,1)S(1)}, bf16[12,24,128]{2,1,0:T(8,128)(2,1)S(1)}, u32[]{:S(2)}, u32[]{:S(2)}) %collective-permute-start.6) | collective-permute-done | bytes 73760 | tf_op jit(solution)/shard_map/ppermute | solution.py:184
  19.1 0.5 %collective-permute-done.7.refs_3_ = bf16[12,24,128]{2,1,0:T(8,128)(2,1)S(1)} collective-permute-done((bf16[12,24,128]{2,1,0:T(8,128)(2,1)S(1)}, bf16[12,24,128]{2,1,0:T(8,128)(2,1)S(1)}, u32[]{:S(2)}, u32[]{:S(2)}) %collective-permute-start.7) | collective-permute-done | bytes 73760 | tf_op jit(solution)/shard_map/ppermute | solution.py:184
  19.6 1.0 %shard_map.82 = bf16[12,24,128]{2,1,0:T(8,128)(2,1)} custom-call(f32[12,24,128]{2,1,0:T(8,128)S(1)} %get-tuple-element.28.refs_0_, bf16[12,24,128]{2,1,0:T(8,128)(2,1)S(1)} %collective-permute-done.5.refs_1_, bf16[12,24,128]{2,1,0:T(8,128)(2,1)S(1)} %collective-permute-done.6.refs_2_, bf16[12,24,128]{2,1,0:T(8,128)(2,1)S(1)} %collective-permute-done.7.refs_3_, ...), custom_call_target="tpu_custom_call" | custom-call | flops 16777216 | bytes 100000 | tf_op jit(solution)/shard_map/pallas_call | solution.py:149
  (1 shorter events, 0.0 us)
Async XLA Ops:
  0.0 4.9 %collective-permute-start = (bf16[12,24,128]{2,1,0:T(8,128)(2,1)}, bf16[12,24,128]{2,1,0:T(8,128)(2,1)S(1)}, u32[]{:S(2)}, u32[]{:S(2)}) collective-permute-start(bf16[12,24,128]{2,1,0:T(8,128)(2,1)} %refs_0_.1), channel_id=1, source_target_pairs={{0,4},{1,5},{2,6},{3,7},{4,0},{5,1},{6,2},{7,3},{8,12},{9,13},{10,... | collective-permute-start | bytes 221192 | tf_op jit(solution)/shard_map/ppermute | solution.py:184
  0.5 6.6 %collective-permute-start.3 = (bf16[12,24,128]{2,1,0:T(8,128)(2,1)}, bf16[12,24,128]{2,1,0:T(8,128)(2,1)S(1)}, u32[]{:S(2)}, u32[]{:S(2)}) collective-permute-start(bf16[12,24,128]{2,1,0:T(8,128)(2,1)} %refs_0_.1), channel_id=1, source_target_pairs={{0,3},{1,2},{2,1},{3,0},{4,7},{5,6},{6,5},{7,4},{8,11},{9,10},{10,... | collective-permute-start | bytes 221192 | tf_op jit(solution)/shard_map/ppermute | solution.py:184
  5.3 4.5 %collective-permute-start.2 = (bf16[288,128]{1,0:T(8,128)(2,1)S(1)}, bf16[288,128]{1,0:T(8,128)(2,1)S(1)}, u32[]{:S(2)}, u32[]{:S(2)}) collective-permute-start(bf16[288,128]{1,0:T(8,128)(2,1)S(1)} %shard_map.74.kept), channel_id=1, source_target_pairs={{0,1},{1,0},{2,3},{3,2},{4,5},{5,4},{6,7},{7,6},{8,9},{9,8},{10,11... | collective-permute-start | bytes 221192 | tf_op jit(solution)/shard_map/ppermute | solution.py:184
  5.9 4.4 %collective-permute-start.1 = (bf16[288,128]{1,0:T(8,128)(2,1)S(1)}, bf16[288,128]{1,0:T(8,128)(2,1)S(1)}, u32[]{:S(2)}, u32[]{:S(2)}) collective-permute-start(bf16[288,128]{1,0:T(8,128)(2,1)S(1)} %shard_map.74.kept), channel_id=1, source_target_pairs={{0,2},{1,3},{2,0},{3,1},{4,6},{5,7},{6,4},{7,5},{8,10},{9,11},{10,... | collective-permute-start | bytes 221192 | tf_op jit(solution)/shard_map/ppermute | solution.py:184
  7.1 1.3 %collective-permute-start.4 = (bf16[144,128]{1,0:T(8,128)(2,1)S(1)}, bf16[144,128]{1,0:T(8,128)(2,1)S(1)}, u32[]{:S(2)}, u32[]{:S(2)}) collective-permute-start(bf16[144,128]{1,0:T(8,128)(2,1)S(1)} %get-tuple-element.25), channel_id=1, source_target_pairs={{0,4},{1,5},{2,6},{3,7},{4,0},{5,1},{6,2},{7,3},{8,12},{9,13},{10,... | collective-permute-start | bytes 110600 | tf_op jit(solution)/shard_map/ppermute | solution.py:184
  10.6 6.0 %collective-permute-start.5 = (bf16[12,24,128]{2,1,0:T(8,128)(2,1)S(1)}, bf16[12,24,128]{2,1,0:T(8,128)(2,1)S(1)}, u32[]{:S(2)}, u32[]{:S(2)}) collective-permute-start(bf16[12,24,128]{2,1,0:T(8,128)(2,1)S(1)} %get-tuple-element.29), channel_id=1, source_target_pairs={{0,8},{1,9},{2,10},{3,11},{4,12},{5,13},{6,14},{7,15},{8,24},{9,25... | collective-permute-start | bytes 221192 | tf_op jit(solution)/shard_map/ppermute | solution.py:184
  12.2 6.9 %collective-permute-start.6 = (bf16[12,24,128]{2,1,0:T(8,128)(2,1)S(1)}, bf16[12,24,128]{2,1,0:T(8,128)(2,1)S(1)}, u32[]{:S(2)}, u32[]{:S(2)}) collective-permute-start(bf16[12,24,128]{2,1,0:T(8,128)(2,1)S(1)} %get-tuple-element.30), channel_id=1, source_target_pairs={{0,24},{1,25},{2,26},{3,27},{4,28},{5,29},{6,30},{7,31},{8,16},{9,... | collective-permute-start | bytes 221192 | tf_op jit(solution)/shard_map/ppermute | solution.py:184
  14.7 4.9 %collective-permute-start.7 = (bf16[12,24,128]{2,1,0:T(8,128)(2,1)S(1)}, bf16[12,24,128]{2,1,0:T(8,128)(2,1)S(1)}, u32[]{:S(2)}, u32[]{:S(2)}) collective-permute-start(bf16[12,24,128]{2,1,0:T(8,128)(2,1)S(1)} %get-tuple-element.31), channel_id=1, source_target_pairs={{0,16},{1,17},{2,18},{3,19},{4,20},{5,21},{6,22},{7,23},{8,0},{9,1... | collective-permute-start | bytes 221192 | tf_op jit(solution)/shard_map/ppermute | solution.py:184

commit v3 on v2

--- a/solution.py
+++ b/solution.py
@@ -71,8 +71,8 @@
     out[...] = jax.nn.sigmoid(dot(ready, weight[...])).reshape(rows, columns, -1)
 
 
-def add_block(left, right, sums, place, start=0, more=False):
-    _, half, columns, width = sums.shape
+def add_block(left, right, sums, start=0, before=None):
+    half, columns, width = sums.shape
     depth = left.shape[0] // half
     group = max(g for g in range(1, half + 1) if half % g == 0 and g * columns <= 288)
     for base in range(0, half, group):
@@ -85,11 +85,11 @@
             )
 
         totals = (jnp.zeros((columns, width), jnp.float32),) * group
-        if more:
-            totals = tuple(sums[place, base + i] for i in range(group))
+        if before is not None:
+            totals = tuple(before[base + i] for i in range(group))
         totals = lax.fori_loop(0, depth, step, totals, unroll=6)
         for i, total in enumerate(totals):
-            sums[place, base + i] = total
+            sums[base + i] = total
 
 
 def first_kernel(kept, mine, other, gain, right_weight, right, sums, left):
@@ -98,28 +98,35 @@
         flat = project(block[...].reshape(rows * columns, width), gain[...], right_weight[...])
         right[pl.ds(part * rows, rows)] = flat.reshape(rows, columns, -1)
     left[...] = kept[...].astype(jnp.float32)
-    add_block(left, right, sums, lax.axis_index("second"))
-
-
-def middle_kernel(steps, *refs):
-    (right, _, sums, left) = refs[len(steps) :]
-    for step, block in zip(steps, refs):
+    add_block(left, right, sums)
+
+
+def middle_kernel(*refs):
+    right, left = refs[0], refs[-1]
+    count = len(refs) // 2 - 1
+    for block, sums in zip(refs[1 : 1 + count], refs[1 + count : -1]):
         left[...] = block[...].astype(jnp.float32)
-        add_block(left, right, sums, lax.axis_index("second") ^ step)
-
-
-def part_kernel(step, more, block, right, gain, weight, _, sums, left):
+        add_block(left, right, sums)
+
+
+def share_kernel(block, right, gain, weight, sums, left):
     left[...] = project(block[...], gain[...], weight[...])
-    start = right.shape[0] // 2 if more else 0
-    add_block(left, right, sums, lax.axis_index("second") ^ step, start, more)
-
-
-def last_kernel(step, messages, merge, block, right, before, *refs):
-    *outs, sums, left = refs
+    add_block(left, right, sums)
+
+
+def joined_kernel(block, right, gain, weight, before, sums, left):
+    left[...] = project(block[...], gain[...], weight[...])
+    add_block(left, right, sums, right.shape[0] // 2, before)
+
+
+def last_kernel(step, steps, messages, merge, block, right, *refs):
+    blocks, outs, (sums, left) = refs[: len(steps)], refs[len(steps) : -2], refs[-2:]
     first, second = lax.axis_index("first"), lax.axis_index("second")
     chip, core = first // 2, lax.rem(first, 2)
+    for at, ready in zip(steps, blocks):
+        sums[second ^ at] = ready[...]
     left[...] = block[...].astype(jnp.float32)
-    add_block(left, right, sums, second ^ step)
+    add_block(left, right, sums.at[second ^ step])
     for out, (targets, cores) in zip(outs, messages):
         place = jnp.int32(0)
         for z, target in enumerate(targets):
@@ -142,7 +149,7 @@
         out[rows] = (result * gate[rows]).astype(out.dtype)
 
 
-def call(kernel, out_shapes, *operands, scratch=(), waits=(), aliases={}, space=pltpu.VMEM):
+def call(kernel, out_shapes, *operands, scratch=(), waits=(), space=pltpu.VMEM):
     many = isinstance(out_shapes, list)
     held = jax.tree.leaves(out_shapes) + list(operands) + list(scratch)
     held = sum(math.prod(ref.shape) * jnp.dtype(ref.dtype).itemsize for ref in held)
@@ -152,7 +159,6 @@
         in_specs=[pl.BlockSpec(memory_space=space)] * len(operands),
         out_specs=[VMEM] * len(out_shapes) if many else VMEM,
         scratch_shapes=[*scratch, *waits],
-        input_output_aliases=aliases,
         compiler_params=pltpu.CompilerParams(vmem_limit_bytes=held + (2 << 20)),
         cost_estimate=pl.CostEstimate(
             flops=1 << 24, bytes_accessed=100000, transcendentals=0
@@ -184,7 +190,7 @@
         return lax.ppermute(values, axes, pairs)
 
     lefts = [pltpu.VMEM((depth * half, mix), f32)]
-    held = shape((seconds, half, columns, mix), f32)
+    held = shape((half, columns, mix), f32)
     part = shape((rows * half, width), pair_rows.dtype)
     other = swap(pair_rows, core=1)
     early = swap(pair_rows, block=seconds - 1)
@@ -216,7 +222,7 @@
     late = list(range(1, seconds - 1))
     blocks = [swap(kept, block=s) for s in late[:-1]]
     last = swap(kept, block=late[-1])
-    right, sums = call(
+    right, own = call(
         first_kernel,
         [shape((depth, columns, mix), f32), held],
         kept,
@@ -229,38 +235,27 @@
     factors = (right, in_gain, left_weight)
     near, passed = call(split_kernel, [part, part], early, scratch=[pltpu.VMEM(part.shape, f32)])
     passed = swap(passed, core=1)
-    for block, more in ((near, False), (passed, True)):
-        sums = call(
-            functools.partial(part_kernel, seconds - 1, more),
-            held,
-            block,
-            *factors,
-            sums,
-            scratch=[pltpu.VMEM((rows * half, mix), f32)],
-            aliases={4: 0},
-        )
-    sums = call(
-        functools.partial(middle_kernel, late[:-1]),
-        held,
-        *blocks,
-        right,
-        sums,
-        scratch=lefts,
-        aliases={len(blocks) + 1: 0},
-    )
+    parts = [pltpu.VMEM((rows * half, mix), f32)]
+    share = call(share_kernel, held, near, *factors, scratch=parts)
+    joined = call(joined_kernel, held, passed, *factors, share, scratch=parts)
+    middle = call(middle_kernel, [held] * len(blocks), right, *blocks, scratch=lefts)
     cores = range(merge)
     messages = [(t, c) for t in [*range(1, chips), 0] for c in reversed(cores)]
-    *outgoing, _ = call(
+    outgoing = call(
         functools.partial(
-            last_kernel, late[-1], [(targets[t], c) for t, c in messages], merge
+            last_kernel,
+            late[-1],
+            [0, seconds - 1, *late[:-1]],
+            [(targets[t], c) for t, c in messages],
+            merge,
         ),
-        [shape((half, columns, mix), f32 if m == (0, 0) else jnp.bfloat16) for m in messages]
-        + [held],
+        [shape((half, columns, mix), f32 if m == (0, 0) else jnp.bfloat16) for m in messages],
         last,
         right,
-        sums,
-        scratch=lefts,
-        aliases={2: len(messages)},
+        own,
+        joined,
+        *middle,
+        scratch=[pltpu.VMEM((seconds, half, columns, mix), f32), *lefts],
     )
     gate = call(gate_kernel, shape((rows, columns, wide), f32), mine, in_gain, out_gate)
     arrived = {

time: 20.7 us -> 20.7 us (level)
  no operation moved by 1% of the time
where the time goes in v3:
time: 20.7 us; the launch traced here: 20.6 us
  starting transfers between devices  10.8 us (52%)
  waiting for transfers between devices  4.91 us (24%)
  Pallas kernels  4.82 us (23%)
    ppermute x8, starting transfers between devices, swap(): return lax.ppermute(values, axes, pairs)  10.8 us
    ppermute x8, waiting for transfers between devices, swap(): return lax.ppermute(values, axes, pairs)  4.91 us
    pallas_call x10, Pallas kernels, call(): pl.pallas_call(kernel, out_shape=out_shapes, in_specs=[pl.BlockSpec(memor...  4.82 us
  transfers between devices with their start and end apart: 8, of which 6 were waited for; matrix products, arithmetic and copies ran while one was open for 0% of the time, Pallas kernels for 17%

profile of v3, /device:TPU:0, one launch (start us, length us, event | category | flops | bytes accessed | tf_op | source)
XLA Modules:
  0.0 20.6 jit_solution(13215839650857271339)
XLA Ops:
  0.0 0.5 %collective-permute-start = (bf16[12,24,128]{2,1,0:T(8,128)(2,1)}, bf16[12,24,128]{2,1,0:T(8,128)(2,1)S(1)}, u32[]{:S(2)}, u32[]{:S(2)}) collective-permute-start(bf16[12,24,128]{2,1,0:T(8,128)(2,1)} %refs_0_.1), channel_id=1, source_target_pairs={{0,4},{1,5},{2,6},{3,7},{4,0},{5,1},{6,2},{7,3},{8,12},{9,13},{10,... | collective-permute-start | bytes 221192 | tf_op jit(solution)/shard_map/ppermute | solution.py:190
  0.5 3.4 %collective-permute-start.2 = (bf16[12,24,128]{2,1,0:T(8,128)(2,1)}, bf16[12,24,128]{2,1,0:T(8,128)(2,1)S(1)}, u32[]{:S(2)}, u32[]{:S(2)}) collective-permute-start(bf16[12,24,128]{2,1,0:T(8,128)(2,1)} %refs_0_.1), channel_id=1, source_target_pairs={{0,3},{1,2},{2,1},{3,0},{4,7},{5,6},{6,5},{7,4},{8,11},{9,10},{10,... | collective-permute-start | bytes 221192 | tf_op jit(solution)/shard_map/ppermute | solution.py:190
  3.9 1.0 %shard_map.73 = (bf16[12,24,128]{2,1,0:T(8,128)(2,1)S(1)}, f32[1,128]{1,0:T(1,128)S(1)}, bf16[128,128]{1,0:T(8,128)(2,1)S(1)}, bf16[128,128]{1,0:T(8,128)(2,1)S(...) custom-call(bf16[12,24,128]{2,1,0:T(8,128)(2,1)} %refs_0_.1, ...), custom_call_target="tpu_custom_call" | custom-call | flops 16777216 | bytes 100000 | tf_op jit(solution)/shard_map/pallas_call | solution.py:156
  4.9 0.0 collective-permute-done.other
  4.9 0.3 %shard_map.74.kept = bf16[288,128]{1,0:T(8,128)(2,1)S(1)} custom-call(bf16[12,24,128]{2,1,0:T(8,128)(2,1)S(1)} %get-tuple-element.20.mine, bf16[12,24,128]{2,1,0:T(8,128)(2,1)S(1)} %collective-permute-done.other, f32[1,128]{1,0:T(1,128)S(1)} %get-tuple-element.21.gain, bf16[128,128]{1,0:T(8,128)(2,1)S(1)} %get-tuple-element.22.weight), custom_call_target="tpu_custom_call" | custom-call | flops 16777216 | bytes 100000 | tf_op jit(solution)/shard_map/pallas_call | solution.py:156
  5.3 0.6 %collective-permute-start.4 = (bf16[288,128]{1,0:T(8,128)(2,1)S(1)}, bf16[288,128]{1,0:T(8,128)(2,1)S(1)}, u32[]{:S(2)}, u32[]{:S(2)}) collective-permute-start(bf16[288,128]{1,0:T(8,128)(2,1)S(1)} %shard_map.74.kept), channel_id=1, source_target_pairs={{0,1},{1,0},{2,3},{3,2},{4,5},{5,4},{6,7},{7,6},{8,9},{9,8},{10,11... | collective-permute-start | bytes 221192 | tf_op jit(solution)/shard_map/ppermute | solution.py:190
  5.9 0.5 %collective-permute-start.1 = (bf16[288,128]{1,0:T(8,128)(2,1)S(1)}, bf16[288,128]{1,0:T(8,128)(2,1)S(1)}, u32[]{:S(2)}, u32[]{:S(2)}) collective-permute-start(bf16[288,128]{1,0:T(8,128)(2,1)S(1)} %shard_map.74.kept), channel_id=1, source_target_pairs={{0,2},{1,3},{2,0},{3,1},{4,6},{5,7},{6,4},{7,5},{8,10},{9,11},{10,... | collective-permute-start | bytes 221192 | tf_op jit(solution)/shard_map/ppermute | solution.py:190
  6.4 0.7 %collective-permute-done.2.block = bf16[12,24,128]{2,1,0:T(8,128)(2,1)S(1)} collective-permute-done((bf16[12,24,128]{2,1,0:T(8,128)(2,1)}, bf16[12,24,128]{2,1,0:T(8,128)(2,1)S(1)}, u32[]{:S(2)}, u32[]{:S(2)}) %collective-permute-start.2) | collective-permute-done | bytes 73760 | tf_op jit(solution)/shard_map/ppermute | solution.py:190
  7.1 0.1 collective-permute-start.3
  7.2 0.6 %shard_map.75 = (f32[24,24,128]{2,1,0:T(8,128)S(1)}, f32[12,24,128]{2,1,0:T(8,128)S(1)}) custom-call(bf16[288,128]{1,0:T(8,128)(2,1)S(1)} %shard_map.74.kept, bf16[12,24,128]{2,1,0:T(8,128)(2,1)S(1)} %get-tuple-element.20.mine, bf16[12,24,128]{2,1,0:T(8,128)(2,1)S(1)} %collective-permute-done.other, f32[1,128]{1,0:T(1,128)S(1)} %get-tuple-element.21.gain, ...), custom_call_target="tpu_custom_call" | custom-call | flops 16777216 | bytes 100000 | tf_op jit(solution)/shard_map/pallas_call | solution.py:156
  7.8 0.4 %shard_map.77.before = f32[12,24,128]{2,1,0:T(8,128)S(1)} custom-call(bf16[144,128]{1,0:T(8,128)(2,1)S(1)} %get-tuple-element.27.block, f32[24,24,128]{2,1,0:T(8,128)S(1)} %get-tuple-element.24.right.refs_0_, f32[1,128]{1,0:T(1,128)S(1)} %get-tuple-element.21.gain, bf16[128,128]{1,0:T(8,128)(2,1)S(1)} %get-tuple-element.22.weight), custom_call_target="tpu_custom_call" | custom-call | flops 16777216 | bytes 100000 | tf_op jit(solution)/shard_map/pallas_call | solution.py:156
  8.3 0.1 collective-permute-done.3.block
  8.4 0.4 %shard_map.78.refs_1_ = f32[12,24,128]{2,1,0:T(8,128)S(1)} custom-call(bf16[144,128]{1,0:T(8,128)(2,1)S(1)} %collective-permute-done.3.block, f32[24,24,128]{2,1,0:T(8,128)S(1)} %get-tuple-element.24.right.refs_0_, f32[1,128]{1,0:T(1,128)S(1)} %get-tuple-element.21.gain, bf16[128,128]{1,0:T(8,128)(2,1)S(1)} %get-tuple-element.22.weight, ...), custom_call_target="tpu_custom_call" | custom-call | flops 16777216 | bytes 100000 | tf_op jit(solution)/shard_map/pallas_call | solution.py:156
  8.8 0.9 %collective-permute-done.4.refs_1_ = bf16[288,128]{1,0:T(8,128)(2,1)S(1)} collective-permute-done((bf16[288,128]{1,0:T(8,128)(2,1)S(1)}, bf16[288,128]{1,0:T(8,128)(2,1)S(1)}, u32[]{:S(2)}, u32[]{:S(2)}) %collective-permute-start.4) | collective-permute-done | bytes 73760 | tf_op jit(solution)/shard_map/ppermute | solution.py:190
  9.8 0.3 %shard_map.79.refs_2_ = f32[12,24,128]{2,1,0:T(8,128)S(1)} custom-call(f32[24,24,128]{2,1,0:T(8,128)S(1)} %get-tuple-element.24.right.refs_0_, bf16[288,128]{1,0:T(8,128)(2,1)S(1)} %collective-permute-done.4.refs_1_), custom_call_target="tpu_custom_call" | custom-call | flops 16777216 | bytes 100000 | tf_op jit(solution)/shard_map/pallas_call | solution.py:156
  10.0 0.2 collective-permute-done.1.block
  10.2 0.3 %shard_map.80 = (bf16[12,24,128]{2,1,0:T(8,128)(2,1)S(1)}, bf16[12,24,128]{2,1,0:T(8,128)(2,1)S(1)}, bf16[12,24,128]{2,1,0:T(8,128)(2,1)S(1)}, f32[12,24,128]{2,1,0:T(8,128)S(1)}) custom-call(bf16[288,128]{1,0:T(8,128)(2,1)S(1)} %collective-permute-done.1.block, f32[24,24,128]{2,1,0:T(8,128)S(1)} %get-tuple-element.24.right.refs_0_, ...), custom_call_target="tpu_custom_call" | custom-call | flops 16777216 | bytes 100000 | tf_op jit(solution)/shard_map/pallas_call | solution.py:156
  10.6 1.6 %collective-permute-start.5 = (bf16[12,24,128]{2,1,0:T(8,128)(2,1)S(1)}, bf16[12,24,128]{2,1,0:T(8,128)(2,1)S(1)}, u32[]{:S(2)}, u32[]{:S(2)}) collective-permute-start(bf16[12,24,128]{2,1,0:T(8,128)(2,1)S(1)} %get-tuple-element.29), channel_id=1, source_target_pairs={{0,8},{1,9},{2,10},{3,11},{4,12},{5,13},{6,14},{7,15},{8,24},{9,25... | collective-permute-start | bytes 221192 | tf_op jit(solution)/shard_map/ppermute | solution.py:190
  12.2 2.5 %collective-permute-start.6 = (bf16[12,24,128]{2,1,0:T(8,128)(2,1)S(1)}, bf16[12,24,128]{2,1,0:T(8,128)(2,1)S(1)}, u32[]{:S(2)}, u32[]{:S(2)}) collective-permute-start(bf16[12,24,128]{2,1,0:T(8,128)(2,1)S(1)} %get-tuple-element.30), channel_id=1, source_target_pairs={{0,24},{1,25},{2,26},{3,27},{4,28},{5,29},{6,30},{7,31},{8,16},{9,... | collective-permute-start | bytes 221192 | tf_op jit(solution)/shard_map/ppermute | solution.py:190
  14.7 1.6 %collective-permute-start.7 = (bf16[12,24,128]{2,1,0:T(8,128)(2,1)S(1)}, bf16[12,24,128]{2,1,0:T(8,128)(2,1)S(1)}, u32[]{:S(2)}, u32[]{:S(2)}) collective-permute-start(bf16[12,24,128]{2,1,0:T(8,128)(2,1)S(1)} %get-tuple-element.31), channel_id=1, source_target_pairs={{0,16},{1,17},{2,18},{3,19},{4,20},{5,21},{6,22},{7,23},{8,0},{9,1... | collective-permute-start | bytes 221192 | tf_op jit(solution)/shard_map/ppermute | solution.py:190
  16.3 0.3 %shard_map.81.refs_4_ = f32[12,24,128]{2,1,0:T(8,128)S(1)} custom-call(bf16[12,24,128]{2,1,0:T(8,128)(2,1)S(1)} %get-tuple-element.20.mine, f32[1,128]{1,0:T(1,128)S(1)} %get-tuple-element.21.gain, bf16[128,128]{1,0:T(8,128)(2,1)S(1)} %get-tuple-element.32.weight), custom_call_target="tpu_custom_call" | custom-call | flops 16777216 | bytes 100000 | tf_op jit(solution)/shard_map/pallas_call | solution.py:156
  16.6 0.0 collective-permute-done.5.refs_1_
  16.6 2.5 %collective-permute-done.6.refs_2_ = bf16[12,24,128]{2,1,0:T(8,128)(2,1)S(1)} collective-permute-done((bf16[12,24,128]{2,1,0:T(8,128)(2,1)S(1)}, bf16[12,24,128]{2,1,0:T(8,128)(2,1)S(1)}, u32[]{:S(2)}, u32[]{:S(2)}) %collective-permute-start.6) | collective-permute-done | bytes 73760 | tf_op jit(solution)/shard_map/ppermute | solution.py:190
  19.1 0.5 %collective-permute-done.7.refs_3_ = bf16[12,24,128]{2,1,0:T(8,128)(2,1)S(1)} collective-permute-done((bf16[12,24,128]{2,1,0:T(8,128)(2,1)S(1)}, bf16[12,24,128]{2,1,0:T(8,128)(2,1)S(1)}, u32[]{:S(2)}, u32[]{:S(2)}) %collective-permute-start.7) | collective-permute-done | bytes 73760 | tf_op jit(solution)/shard_map/ppermute | solution.py:190
  19.6 1.0 %shard_map.82 = bf16[12,24,128]{2,1,0:T(8,128)(2,1)} custom-call(f32[12,24,128]{2,1,0:T(8,128)S(1)} %get-tuple-element.28.refs_0_, bf16[12,24,128]{2,1,0:T(8,128)(2,1)S(1)} %collective-permute-done.5.refs_1_, bf16[12,24,128]{2,1,0:T(8,128)(2,1)S(1)} %collective-permute-done.6.refs_2_, bf16[12,24,128]{2,1,0:T(8,128)(2,1)S(1)} %collective-permute-done.7.refs_3_, ...), custom_call_target="tpu_custom_call" | custom-call | flops 16777216 | bytes 100000 | tf_op jit(solution)/shard_map/pallas_call | solution.py:156
  (1 shorter events, 0.0 us)
Async XLA Ops:
  0.0 4.9 %collective-permute-start = (bf16[12,24,128]{2,1,0:T(8,128)(2,1)}, bf16[12,24,128]{2,1,0:T(8,128)(2,1)S(1)}, u32[]{:S(2)}, u32[]{:S(2)}) collective-permute-start(bf16[12,24,128]{2,1,0:T(8,128)(2,1)} %refs_0_.1), channel_id=1, source_target_pairs={{0,4},{1,5},{2,6},{3,7},{4,0},{5,1},{6,2},{7,3},{8,12},{9,13},{10,... | collective-permute-start | bytes 221192 | tf_op jit(solution)/shard_map/ppermute | solution.py:190
  0.5 6.6 %collective-permute-start.2 = (bf16[12,24,128]{2,1,0:T(8,128)(2,1)}, bf16[12,24,128]{2,1,0:T(8,128)(2,1)S(1)}, u32[]{:S(2)}, u32[]{:S(2)}) collective-permute-start(bf16[12,24,128]{2,1,0:T(8,128)(2,1)} %refs_0_.1), channel_id=1, source_target_pairs={{0,3},{1,2},{2,1},{3,0},{4,7},{5,6},{6,5},{7,4},{8,11},{9,10},{10,... | collective-permute-start | bytes 221192 | tf_op jit(solution)/shard_map/ppermute | solution.py:190
  5.3 4.5 %collective-permute-start.4 = (bf16[288,128]{1,0:T(8,128)(2,1)S(1)}, bf16[288,128]{1,0:T(8,128)(2,1)S(1)}, u32[]{:S(2)}, u32[]{:S(2)}) collective-permute-start(bf16[288,128]{1,0:T(8,128)(2,1)S(1)} %shard_map.74.kept), channel_id=1, source_target_pairs={{0,1},{1,0},{2,3},{3,2},{4,5},{5,4},{6,7},{7,6},{8,9},{9,8},{10,11... | collective-permute-start | bytes 221192 | tf_op jit(solution)/shard_map/ppermute | solution.py:190
  5.9 4.4 %collective-permute-start.1 = (bf16[288,128]{1,0:T(8,128)(2,1)S(1)}, bf16[288,128]{1,0:T(8,128)(2,1)S(1)}, u32[]{:S(2)}, u32[]{:S(2)}) collective-permute-start(bf16[288,128]{1,0:T(8,128)(2,1)S(1)} %shard_map.74.kept), channel_id=1, source_target_pairs={{0,2},{1,3},{2,0},{3,1},{4,6},{5,7},{6,4},{7,5},{8,10},{9,11},{10,... | collective-permute-start | bytes 221192 | tf_op jit(solution)/shard_map/ppermute | solution.py:190
  7.1 1.3 %collective-permute-start.3 = (bf16[144,128]{1,0:T(8,128)(2,1)S(1)}, bf16[144,128]{1,0:T(8,128)(2,1)S(1)}, u32[]{:S(2)}, u32[]{:S(2)}) collective-permute-start(bf16[144,128]{1,0:T(8,128)(2,1)S(1)} %get-tuple-element.26), channel_id=1, source_target_pairs={{0,4},{1,5},{2,6},{3,7},{4,0},{5,1},{6,2},{7,3},{8,12},{9,13},{10,... | collective-permute-start | bytes 110600 | tf_op jit(solution)/shard_map/ppermute | solution.py:190
  10.6 6.0 %collective-permute-start.5 = (bf16[12,24,128]{2,1,0:T(8,128)(2,1)S(1)}, bf16[12,24,128]{2,1,0:T(8,128)(2,1)S(1)}, u32[]{:S(2)}, u32[]{:S(2)}) collective-permute-start(bf16[12,24,128]{2,1,0:T(8,128)(2,1)S(1)} %get-tuple-element.29), channel_id=1, source_target_pairs={{0,8},{1,9},{2,10},{3,11},{4,12},{5,13},{6,14},{7,15},{8,24},{9,25... | collective-permute-start | bytes 221192 | tf_op jit(solution)/shard_map/ppermute | solution.py:190
  12.2 6.9 %collective-permute-start.6 = (bf16[12,24,128]{2,1,0:T(8,128)(2,1)S(1)}, bf16[12,24,128]{2,1,0:T(8,128)(2,1)S(1)}, u32[]{:S(2)}, u32[]{:S(2)}) collective-permute-start(bf16[12,24,128]{2,1,0:T(8,128)(2,1)S(1)} %get-tuple-element.30), channel_id=1, source_target_pairs={{0,24},{1,25},{2,26},{3,27},{4,28},{5,29},{6,30},{7,31},{8,16},{9,... | collective-permute-start | bytes 221192 | tf_op jit(solution)/shard_map/ppermute | solution.py:190
  14.7 4.9 %collective-permute-start.7 = (bf16[12,24,128]{2,1,0:T(8,128)(2,1)S(1)}, bf16[12,24,128]{2,1,0:T(8,128)(2,1)S(1)}, u32[]{:S(2)}, u32[]{:S(2)}) collective-permute-start(bf16[12,24,128]{2,1,0:T(8,128)(2,1)S(1)} %get-tuple-element.31), channel_id=1, source_target_pairs={{0,16},{1,17},{2,18},{3,19},{4,20},{5,21},{6,22},{7,23},{8,0},{9,1... | collective-permute-start | bytes 221192 | tf_op jit(solution)/shard_map/ppermute | solution.py:190

commit v4 on v3

--- a/solution.py
+++ b/solution.py
@@ -87,7 +87,7 @@
         totals = (jnp.zeros((columns, width), jnp.float32),) * group
         if before is not None:
             totals = tuple(before[base + i] for i in range(group))
-        totals = lax.fori_loop(0, depth, step, totals, unroll=6)
+        totals = lax.fori_loop(0, depth, step, totals, unroll=12)
         for i, total in enumerate(totals):
             sums[base + i] = total
 
@@ -133,6 +133,10 @@
             place = jnp.where(chip == z, target, place)
         place = place if merge == 1 else 2 * place + (core ^ cores)
         out[...] = sums[place].astype(out.dtype)
+
+
+def presum_kernel(*refs):
+    refs[-1][...] = sum(part[...].astype(jnp.float32) for part in refs[:-1])
 
 
 def final_kernel(merge, per, scale, *refs):
@@ -262,9 +266,12 @@
         (t, c): sent if (t, c) == (0, 0) else swap(sent, step=t, core=c)
         for (t, c), sent in zip(messages, outgoing)
     }
-    parts = [arrived[t, c] for c in cores for t in range(chips)]
+    parts = []
+    for c in cores:
+        *ready, latest = [arrived[t, c] for t in range(chips)]
+        parts += [call(presum_kernel, held, *ready), latest]
     return call(
-        functools.partial(final_kernel, merge, chips, (rows * firsts) ** -0.5),
+        functools.partial(final_kernel, merge, 2, (rows * firsts) ** -0.5),
         shape((rows, columns, wide), jnp.bfloat16),
         *parts,
         gate,

time: 20.7 us -> 20.7 us (level)
    pallas_call x10 -> x11, Pallas kernels: 4.82 us -> 4.76 us  [call(): pl.pallas_call(kernel, out_shape=out_shapes, in_specs=[pl.BlockSpec(memor...]
where the time goes in v4:
time: 20.7 us; the launch traced here: 20.6 us
  starting transfers between devices  10.8 us (52%)
  waiting for transfers between devices  4.94 us (24%)
  Pallas kernels  4.76 us (23%)
    ppermute x8, starting transfers between devices, swap(): return lax.ppermute(values, axes, pairs)  10.8 us
    ppermute x8, waiting for transfers between devices, swap(): return lax.ppermute(values, axes, pairs)  4.94 us
    pallas_call x11, Pallas kernels, call(): pl.pallas_call(kernel, out_shape=out_shapes, in_specs=[pl.BlockSpec(memor...  4.76 us
  transfers between devices with their start and end apart: 8, of which 6 were waited for; matrix products, arithmetic and copies ran while one was open for 0% of the time, Pallas kernels for 17%

profile of v4, /device:TPU:0, one launch (start us, length us, event | category | flops | bytes accessed | tf_op | source)
XLA Modules:
  0.0 20.6 jit_solution(5153384874373662584)
XLA Ops:
  0.0 0.5 %collective-permute-start = (bf16[12,24,128]{2,1,0:T(8,128)(2,1)}, bf16[12,24,128]{2,1,0:T(8,128)(2,1)S(1)}, u32[]{:S(2)}, u32[]{:S(2)}) collective-permute-start(bf16[12,24,128]{2,1,0:T(8,128)(2,1)} %refs_0_.1), channel_id=1, source_target_pairs={{0,4},{1,5},{2,6},{3,7},{4,0},{5,1},{6,2},{7,3},{8,12},{9,13},{10,... | collective-permute-start | bytes 221192 | tf_op jit(solution)/shard_map/ppermute | solution.py:194
  0.5 3.4 %collective-permute-start.2 = (bf16[12,24,128]{2,1,0:T(8,128)(2,1)}, bf16[12,24,128]{2,1,0:T(8,128)(2,1)S(1)}, u32[]{:S(2)}, u32[]{:S(2)}) collective-permute-start(bf16[12,24,128]{2,1,0:T(8,128)(2,1)} %refs_0_.1), channel_id=1, source_target_pairs={{0,3},{1,2},{2,1},{3,0},{4,7},{5,6},{6,5},{7,4},{8,11},{9,10},{10,... | collective-permute-start | bytes 221192 | tf_op jit(solution)/shard_map/ppermute | solution.py:194
  3.9 1.0 %shard_map.73 = (bf16[12,24,128]{2,1,0:T(8,128)(2,1)S(1)}, f32[1,128]{1,0:T(1,128)S(1)}, bf16[128,128]{1,0:T(8,128)(2,1)S(1)}, bf16[128,128]{1,0:T(8,128)(2,1)S(...) custom-call(bf16[12,24,128]{2,1,0:T(8,128)(2,1)} %refs_0_.1, ...), custom_call_target="tpu_custom_call" | custom-call | flops 16777216 | bytes 100000 | tf_op jit(solution)/shard_map/pallas_call | solution.py:160
  4.9 0.0 collective-permute-done.other
  4.9 0.3 %shard_map.74.kept = bf16[288,128]{1,0:T(8,128)(2,1)S(1)} custom-call(bf16[12,24,128]{2,1,0:T(8,128)(2,1)S(1)} %get-tuple-element.20.mine, bf16[12,24,128]{2,1,0:T(8,128)(2,1)S(1)} %collective-permute-done.other, f32[1,128]{1,0:T(1,128)S(1)} %get-tuple-element.21.gain, bf16[128,128]{1,0:T(8,128)(2,1)S(1)} %get-tuple-element.22.weight), custom_call_target="tpu_custom_call" | custom-call | flops 16777216 | bytes 100000 | tf_op jit(solution)/shard_map/pallas_call | solution.py:160
  5.3 0.6 %collective-permute-start.4 = (bf16[288,128]{1,0:T(8,128)(2,1)S(1)}, bf16[288,128]{1,0:T(8,128)(2,1)S(1)}, u32[]{:S(2)}, u32[]{:S(2)}) collective-permute-start(bf16[288,128]{1,0:T(8,128)(2,1)S(1)} %shard_map.74.kept), channel_id=1, source_target_pairs={{0,1},{1,0},{2,3},{3,2},{4,5},{5,4},{6,7},{7,6},{8,9},{9,8},{10,11... | collective-permute-start | bytes 221192 | tf_op jit(solution)/shard_map/ppermute | solution.py:194
  5.9 0.5 %collective-permute-start.1 = (bf16[288,128]{1,0:T(8,128)(2,1)S(1)}, bf16[288,128]{1,0:T(8,128)(2,1)S(1)}, u32[]{:S(2)}, u32[]{:S(2)}) collective-permute-start(bf16[288,128]{1,0:T(8,128)(2,1)S(1)} %shard_map.74.kept), channel_id=1, source_target_pairs={{0,2},{1,3},{2,0},{3,1},{4,6},{5,7},{6,4},{7,5},{8,10},{9,11},{10,... | collective-permute-start | bytes 221192 | tf_op jit(solution)/shard_map/ppermute | solution.py:194
  6.4 0.7 %collective-permute-done.2.block = bf16[12,24,128]{2,1,0:T(8,128)(2,1)S(1)} collective-permute-done((bf16[12,24,128]{2,1,0:T(8,128)(2,1)}, bf16[12,24,128]{2,1,0:T(8,128)(2,1)S(1)}, u32[]{:S(2)}, u32[]{:S(2)}) %collective-permute-start.2) | collective-permute-done | bytes 73760 | tf_op jit(solution)/shard_map/ppermute | solution.py:194
  7.1 0.1 collective-permute-start.3
  7.2 0.6 %shard_map.75 = (f32[24,24,128]{2,1,0:T(8,128)S(1)}, f32[12,24,128]{2,1,0:T(8,128)S(1)}) custom-call(bf16[288,128]{1,0:T(8,128)(2,1)S(1)} %shard_map.74.kept, bf16[12,24,128]{2,1,0:T(8,128)(2,1)S(1)} %get-tuple-element.20.mine, bf16[12,24,128]{2,1,0:T(8,128)(2,1)S(1)} %collective-permute-done.other, f32[1,128]{1,0:T(1,128)S(1)} %get-tuple-element.21.gain, ...), custom_call_target="tpu_custom_call" | custom-call | flops 16777216 | bytes 100000 | tf_op jit(solution)/shard_map/pallas_call | solution.py:160
  7.8 0.4 %shard_map.77.before = f32[12,24,128]{2,1,0:T(8,128)S(1)} custom-call(bf16[144,128]{1,0:T(8,128)(2,1)S(1)} %get-tuple-element.27.block, f32[24,24,128]{2,1,0:T(8,128)S(1)} %get-tuple-element.24.right.refs_0_, f32[1,128]{1,0:T(1,128)S(1)} %get-tuple-element.21.gain, bf16[128,128]{1,0:T(8,128)(2,1)S(1)} %get-tuple-element.22.weight), custom_call_target="tpu_custom_call" | custom-call | flops 16777216 | bytes 100000 | tf_op jit(solution)/shard_map/pallas_call | solution.py:160
  8.3 0.1 collective-permute-done.3.block
  8.4 0.4 %shard_map.78.refs_1_ = f32[12,24,128]{2,1,0:T(8,128)S(1)} custom-call(bf16[144,128]{1,0:T(8,128)(2,1)S(1)} %collective-permute-done.3.block, f32[24,24,128]{2,1,0:T(8,128)S(1)} %get-tuple-element.24.right.refs_0_, f32[1,128]{1,0:T(1,128)S(1)} %get-tuple-element.21.gain, bf16[128,128]{1,0:T(8,128)(2,1)S(1)} %get-tuple-element.22.weight, ...), custom_call_target="tpu_custom_call" | custom-call | flops 16777216 | bytes 100000 | tf_op jit(solution)/shard_map/pallas_call | solution.py:160
  8.8 0.9 %collective-permute-done.4.refs_1_ = bf16[288,128]{1,0:T(8,128)(2,1)S(1)} collective-permute-done((bf16[288,128]{1,0:T(8,128)(2,1)S(1)}, bf16[288,128]{1,0:T(8,128)(2,1)S(1)}, u32[]{:S(2)}, u32[]{:S(2)}) %collective-permute-start.4) | collective-permute-done | bytes 73760 | tf_op jit(solution)/shard_map/ppermute | solution.py:194
  9.8 0.3 %shard_map.79.refs_2_ = f32[12,24,128]{2,1,0:T(8,128)S(1)} custom-call(f32[24,24,128]{2,1,0:T(8,128)S(1)} %get-tuple-element.24.right.refs_0_, bf16[288,128]{1,0:T(8,128)(2,1)S(1)} %collective-permute-done.4.refs_1_), custom_call_target="tpu_custom_call" | custom-call | flops 16777216 | bytes 100000 | tf_op jit(solution)/shard_map/pallas_call | solution.py:160
  10.0 0.2 %collective-permute-done.1.block = bf16[288,128]{1,0:T(8,128)(2,1)S(1)} collective-permute-done((bf16[288,128]{1,0:T(8,128)(2,1)S(1)}, bf16[288,128]{1,0:T(8,128)(2,1)S(1)}, u32[]{:S(2)}, u32[]{:S(2)}) %collective-permute-start.1) | collective-permute-done | bytes 73760 | tf_op jit(solution)/shard_map/ppermute | solution.py:194
  10.2 0.3 %shard_map.80 = (bf16[12,24,128]{2,1,0:T(8,128)(2,1)S(1)}, bf16[12,24,128]{2,1,0:T(8,128)(2,1)S(1)}, bf16[12,24,128]{2,1,0:T(8,128)(2,1)S(1)}, f32[12,24,128]{2,1,0:T(8,128)S(1)}) custom-call(bf16[288,128]{1,0:T(8,128)(2,1)S(1)} %collective-permute-done.1.block, f32[24,24,128]{2,1,0:T(8,128)S(1)} %get-tuple-element.24.right.refs_0_, ...), custom_call_target="tpu_custom_call" | custom-call | flops 16777216 | bytes 100000 | tf_op jit(solution)/shard_map/pallas_call | solution.py:160
  10.6 1.6 %collective-permute-start.5 = (bf16[12,24,128]{2,1,0:T(8,128)(2,1)S(1)}, bf16[12,24,128]{2,1,0:T(8,128)(2,1)S(1)}, u32[]{:S(2)}, u32[]{:S(2)}) collective-permute-start(bf16[12,24,128]{2,1,0:T(8,128)(2,1)S(1)} %get-tuple-element.29), channel_id=1, source_target_pairs={{0,8},{1,9},{2,10},{3,11},{4,12},{5,13},{6,14},{7,15},{8,24},{9,25... | collective-permute-start | bytes 221192 | tf_op jit(solution)/shard_map/ppermute | solution.py:194
  12.2 2.5 %collective-permute-start.6 = (bf16[12,24,128]{2,1,0:T(8,128)(2,1)S(1)}, bf16[12,24,128]{2,1,0:T(8,128)(2,1)S(1)}, u32[]{:S(2)}, u32[]{:S(2)}) collective-permute-start(bf16[12,24,128]{2,1,0:T(8,128)(2,1)S(1)} %get-tuple-element.30), channel_id=1, source_target_pairs={{0,24},{1,25},{2,26},{3,27},{4,28},{5,29},{6,30},{7,31},{8,16},{9,... | collective-permute-start | bytes 221192 | tf_op jit(solution)/shard_map/ppermute | solution.py:194
  14.7 1.6 %collective-permute-start.7 = (bf16[12,24,128]{2,1,0:T(8,128)(2,1)S(1)}, bf16[12,24,128]{2,1,0:T(8,128)(2,1)S(1)}, u32[]{:S(2)}, u32[]{:S(2)}) collective-permute-start(bf16[12,24,128]{2,1,0:T(8,128)(2,1)S(1)} %get-tuple-element.31), channel_id=1, source_target_pairs={{0,16},{1,17},{2,18},{3,19},{4,20},{5,21},{6,22},{7,23},{8,0},{9,1... | collective-permute-start | bytes 221192 | tf_op jit(solution)/shard_map/ppermute | solution.py:194
  16.3 0.3 %shard_map.82.refs_2_ = f32[12,24,128]{2,1,0:T(8,128)S(1)} custom-call(bf16[12,24,128]{2,1,0:T(8,128)(2,1)S(1)} %get-tuple-element.20.mine, f32[1,128]{1,0:T(1,128)S(1)} %get-tuple-element.21.gain, bf16[128,128]{1,0:T(8,128)(2,1)S(1)} %get-tuple-element.32.weight), custom_call_target="tpu_custom_call" | custom-call | flops 16777216 | bytes 100000 | tf_op jit(solution)/shard_map/pallas_call | solution.py:160
  16.6 0.0 collective-permute-done.5.refs_1_
  16.6 2.4 %collective-permute-done.6.refs_2_ = bf16[12,24,128]{2,1,0:T(8,128)(2,1)S(1)} collective-permute-done((bf16[12,24,128]{2,1,0:T(8,128)(2,1)S(1)}, bf16[12,24,128]{2,1,0:T(8,128)(2,1)S(1)}, u32[]{:S(2)}, u32[]{:S(2)}) %collective-permute-start.6) | collective-permute-done | bytes 73760 | tf_op jit(solution)/shard_map/ppermute | solution.py:194
  19.1 0.5 %collective-permute-done.7.refs_1_ = bf16[12,24,128]{2,1,0:T(8,128)(2,1)S(1)} collective-permute-done((bf16[12,24,128]{2,1,0:T(8,128)(2,1)S(1)}, bf16[12,24,128]{2,1,0:T(8,128)(2,1)S(1)}, u32[]{:S(2)}, u32[]{:S(2)}) %collective-permute-start.7) | collective-permute-done | bytes 73760 | tf_op jit(solution)/shard_map/ppermute | solution.py:194
  19.6 1.0 %shard_map.83 = bf16[12,24,128]{2,1,0:T(8,128)(2,1)} custom-call(f32[12,24,128]{2,1,0:T(8,128)S(1)} %shard_map.81.refs_0_, bf16[12,24,128]{2,1,0:T(8,128)(2,1)S(1)} %collective-permute-done.7.refs_1_, f32[12,24,128]{2,1,0:T(8,128)S(1)} %shard_map.82.refs_2_, f32[1,128]{1,0:T(1,128)S(1)} %get-tuple-element.33.refs_3_, ...), custom_call_target="tpu_custom_call" | custom-call | flops 16777216 | bytes 100000 | tf_op jit(solution)/shard_map/pallas_call | solution.py:160
  (2 shorter events, 0.1 us)
Async XLA Ops:
  0.0 4.9 %collective-permute-start = (bf16[12,24,128]{2,1,0:T(8,128)(2,1)}, bf16[12,24,128]{2,1,0:T(8,128)(2,1)S(1)}, u32[]{:S(2)}, u32[]{:S(2)}) collective-permute-start(bf16[12,24,128]{2,1,0:T(8,128)(2,1)} %refs_0_.1), channel_id=1, source_target_pairs={{0,4},{1,5},{2,6},{3,7},{4,0},{5,1},{6,2},{7,3},{8,12},{9,13},{10,... | collective-permute-start | bytes 221192 | tf_op jit(solution)/shard_map/ppermute | solution.py:194
  0.5 6.6 %collective-permute-start.2 = (bf16[12,24,128]{2,1,0:T(8,128)(2,1)}, bf16[12,24,128]{2,1,0:T(8,128)(2,1)S(1)}, u32[]{:S(2)}, u32[]{:S(2)}) collective-permute-start(bf16[12,24,128]{2,1,0:T(8,128)(2,1)} %refs_0_.1), channel_id=1, source_target_pairs={{0,3},{1,2},{2,1},{3,0},{4,7},{5,6},{6,5},{7,4},{8,11},{9,10},{10,... | collective-permute-start | bytes 221192 | tf_op jit(solution)/shard_map/ppermute | solution.py:194
  5.3 4.5 %collective-permute-start.4 = (bf16[288,128]{1,0:T(8,128)(2,1)S(1)}, bf16[288,128]{1,0:T(8,128)(2,1)S(1)}, u32[]{:S(2)}, u32[]{:S(2)}) collective-permute-start(bf16[288,128]{1,0:T(8,128)(2,1)S(1)} %shard_map.74.kept), channel_id=1, source_target_pairs={{0,1},{1,0},{2,3},{3,2},{4,5},{5,4},{6,7},{7,6},{8,9},{9,8},{10,11... | collective-permute-start | bytes 221192 | tf_op jit(solution)/shard_map/ppermute | solution.py:194
  5.9 4.4 %collective-permute-start.1 = (bf16[288,128]{1,0:T(8,128)(2,1)S(1)}, bf16[288,128]{1,0:T(8,128)(2,1)S(1)}, u32[]{:S(2)}, u32[]{:S(2)}) collective-permute-start(bf16[288,128]{1,0:T(8,128)(2,1)S(1)} %shard_map.74.kept), channel_id=1, source_target_pairs={{0,2},{1,3},{2,0},{3,1},{4,6},{5,7},{6,4},{7,5},{8,10},{9,11},{10,... | collective-permute-start | bytes 221192 | tf_op jit(solution)/shard_map/ppermute | solution.py:194
  7.1 1.3 %collective-permute-start.3 = (bf16[144,128]{1,0:T(8,128)(2,1)S(1)}, bf16[144,128]{1,0:T(8,128)(2,1)S(1)}, u32[]{:S(2)}, u32[]{:S(2)}) collective-permute-start(bf16[144,128]{1,0:T(8,128)(2,1)S(1)} %get-tuple-element.26), channel_id=1, source_target_pairs={{0,4},{1,5},{2,6},{3,7},{4,0},{5,1},{6,2},{7,3},{8,12},{9,13},{10,... | collective-permute-start | bytes 110600 | tf_op jit(solution)/shard_map/ppermute | solution.py:194
  10.6 6.0 %collective-permute-start.5 = (bf16[12,24,128]{2,1,0:T(8,128)(2,1)S(1)}, bf16[12,24,128]{2,1,0:T(8,128)(2,1)S(1)}, u32[]{:S(2)}, u32[]{:S(2)}) collective-permute-start(bf16[12,24,128]{2,1,0:T(8,128)(2,1)S(1)} %get-tuple-element.29), channel_id=1, source_target_pairs={{0,8},{1,9},{2,10},{3,11},{4,12},{5,13},{6,14},{7,15},{8,24},{9,25... | collective-permute-start | bytes 221192 | tf_op jit(solution)/shard_map/ppermute | solution.py:194
  12.2 6.8 %collective-permute-start.6 = (bf16[12,24,128]{2,1,0:T(8,128)(2,1)S(1)}, bf16[12,24,128]{2,1,0:T(8,128)(2,1)S(1)}, u32[]{:S(2)}, u32[]{:S(2)}) collective-permute-start(bf16[12,24,128]{2,1,0:T(8,128)(2,1)S(1)} %get-tuple-element.30), channel_id=1, source_target_pairs={{0,24},{1,25},{2,26},{3,27},{4,28},{5,29},{6,30},{7,31},{8,16},{9,... | collective-permute-start | bytes 221192 | tf_op jit(solution)/shard_map/ppermute | solution.py:194
  14.7 4.9 %collective-permute-start.7 = (bf16[12,24,128]{2,1,0:T(8,128)(2,1)S(1)}, bf16[12,24,128]{2,1,0:T(8,128)(2,1)S(1)}, u32[]{:S(2)}, u32[]{:S(2)}) collective-permute-start(bf16[12,24,128]{2,1,0:T(8,128)(2,1)S(1)} %get-tuple-element.31), channel_id=1, source_target_pairs={{0,16},{1,17},{2,18},{3,19},{4,20},{5,21},{6,22},{7,23},{8,0},{9,1... | collective-permute-start | bytes 221192 | tf_op jit(solution)/shard_map/ppermute | solution.py:194
